TPU v7x, 32 devices: a 4x2x2 block of a 4x4x8 slice. The times are simulated.
32 devices in a mesh: rep: 4 (over y, z), data: 8 (over x, core).
Axes of the slice: x: 4, y: 2, z: 2, core: 2. Of those that a mesh axis runs over, the one named last changes fastest.
The devices are a block of a 4x4x8 slice.
Arguments:
- W_in: float32 [16384, 1024], P('rep'), parts along dimension 0
- W1: float32 [4, 1024, 4096], P('rep'), parts along dimension 0
- W2: float32 [4, 4096, 1024], P('rep'), parts along dimension 0
- m_in: float32 [16384, 1024], P('rep'), parts along dimension 0
- v_in: float32 [16384, 1024], P('rep'), parts along dimension 0
- m1: float32 [4, 1024, 4096], P('rep'), parts along dimension 0
- v1: float32 [4, 1024, 4096], P('rep'), parts along dimension 0
- m2: float32 [4, 4096, 1024], P('rep'), parts along dimension 0
- v2: float32 [4, 4096, 1024], P('rep'), parts along dimension 0
- X0: bfloat16 [8192, 4096], P(('rep', 'data')), parts along dimension 0
- Y0: bfloat16 [8192, 1024], P(('rep', 'data')), parts along dimension 0
- X1: bfloat16 [8192, 4096], P(('rep', 'data')), parts along dimension 0
- Y1: bfloat16 [8192, 1024], P(('rep', 'data')), parts along dimension 0
Outputs:
- output 1: float32 [16384, 1024], P('rep'), parts along dimension 0
- output 2: float32 [4, 1024, 4096], P('rep'), parts along dimension 0
- output 3: float32 [4, 4096, 1024], P('rep'), parts along dimension 0
- output 4: float32 [16384, 1024], P('rep'), parts along dimension 0
- output 5: float32 [16384, 1024], P('rep'), parts along dimension 0
- output 6: float32 [4, 1024, 4096], P('rep'), parts along dimension 0
- output 7: float32 [4, 1024, 4096], P('rep'), parts along dimension 0
- output 8: float32 [4, 4096, 1024], P('rep'), parts along dimension 0
- output 9: float32 [4, 4096, 1024], P('rep'), parts along dimension 0
- output 10: float32 [8192], P(('rep', 'data')), parts along dimension 0
- output 11: float32 [8192, 1024], P(('rep', 'data')), parts along dimension 0
There are 4 independent parts. A program takes and returns all parts, laid end to end along the dimension named above; each array names one.
All inputs are finite; a program needn't handle non-finite values.
Results may differ from a plain program's by a relative error of at most 0.0174769.
Values are sent between devices in bfloat16 or wider.
A program may use at most 768 MiB of HBM per device.

v0:
```python
import jax
import jax.numpy as jnp
from jax import lax
from jax.sharding import PartitionSpec as P

BETA1 = 0.9
BETA2 = 0.999
BC1 = 1.0 / (1.0 - BETA1 ** 10)
BC2 = 1.0 / (1.0 - BETA2 ** 10)
EPS = 1e-12
WD = 0.01
ETA = 0.05
R2 = 0.7071067811865476
R2PI = 0.3989422804014327
BF = jnp.bfloat16
F32 = jnp.float32


def gelu_grad(a):
    return 0.5 * (1.0 + lax.erf(a * R2)) + a * jnp.exp(-0.5 * a * a) * R2PI


def lamb(w, g, m, v):
    m2 = BETA1 * m + (1.0 - BETA1) * g
    v2 = BETA2 * v + (1.0 - BETA2) * g * g
    u = BC1 * m2 / (jnp.sqrt(BC2 * v2) + EPS) + WD * w
    r = jnp.sqrt(jnp.sum(w * w)) / jnp.sqrt(jnp.sum(u * u))
    return w - ETA * r * u, m2, v2


def group_sum(g, p):
    rows, cols = g.shape
    got = lax.all_to_all(g, 'data', 0, 0, tiled=True).reshape(p, rows // p, cols)
    s = jnp.sum(got, axis=0, dtype=F32).astype(BF)
    return lax.all_gather(s, 'data', axis=0, tiled=True).astype(F32)


def forward(wib, w1b, w2b, x):
    h = jnp.dot(x, wib, preferred_element_type=F32)
    for l in range(len(w1b)):
        s = jax.nn.gelu(jnp.dot(h.astype(BF), w1b[l], preferred_element_type=F32), approximate=False).astype(BF)
        h = h + jnp.dot(s, w2b[l], preferred_element_type=F32)
    return h


def stacked(ups, k):
    return jnp.stack([u[k] for u in ups])


def solution(mesh):
    p = mesh.shape['data']

    def step(wi, w1, w2, mi, vi, m1, v1, m2, v2, x0, y0, x1, y1):
        nl = w1.shape[0]
        d = wi.shape[1]
        scale = 1.0 / (x0.shape[0] * p * d)
        wib = wi.astype(BF)
        w1b = [w1[l].astype(BF) for l in range(nl)]
        w2b = [w2[l].astype(BF) for l in range(nl)]
        h = jnp.dot(x0, wib, preferred_element_type=F32)
        saved = []
        for l in range(nl):
            a = jnp.dot(h.astype(BF), w1b[l], preferred_element_type=F32)
            s = jax.nn.gelu(a, approximate=False).astype(BF)
            saved.append((h.astype(BF), a, s))
            h = h + jnp.dot(s, w2b[l], preferred_element_type=F32)
        g = (h - y0.astype(F32)) * scale
        dw1 = [None] * nl
        dw2 = [None] * nl
        for l in reversed(range(nl)):
            hb, a, s = saved[l]
            gb = g.astype(BF)
            dw2[l] = jnp.dot(s.T, gb, preferred_element_type=F32).astype(BF)
            e = (jnp.dot(gb, w2b[l].T, preferred_element_type=F32) * gelu_grad(a)).astype(BF)
            dw1[l] = jnp.dot(hb.T, e, preferred_element_type=F32).astype(BF)
            g = g + jnp.dot(e, w1b[l].T, preferred_element_type=F32)
        dwi = jnp.dot(x0.T, g.astype(BF), preferred_element_type=F32).astype(BF)
        s1 = [None] * nl
        s2 = [None] * nl
        for l in reversed(range(nl)):
            s2[l] = group_sum(dw2[l], p)
            s1[l] = group_sum(dw1[l], p)
        si = group_sum(dwi, p)
        wi_n, mi_n, vi_n = lamb(wi, si, mi, vi)
        up1 = [lamb(w1[l], s1[l], m1[l], v1[l]) for l in range(nl)]
        up2 = [lamb(w2[l], s2[l], m2[l], v2[l]) for l in range(nl)]
        h1 = forward(wi_n.astype(BF), [u[0].astype(BF) for u in up1], [u[0].astype(BF) for u in up2], x1)
        loss = jnp.sum((h1 - y1.astype(F32)) ** 2, axis=-1) / (2.0 * d)
        return (wi_n, stacked(up1, 0), stacked(up2, 0), mi_n, vi_n,
                stacked(up1, 1), stacked(up1, 2), stacked(up2, 1), stacked(up2, 2), loss, h1)

    w2s = P('rep', None)
    w3s = P('rep', None, None)
    ts = P(('rep', 'data'), None)
    return jax.shard_map(step, mesh=mesh,
                         in_specs=(w2s, w3s, w3s, w2s, w2s, w3s, w3s, w3s, w3s, ts, ts, ts, ts),
                         out_specs=(w2s, w3s, w3s, w2s, w2s, w3s, w3s, w3s, w3s, P(('rep', 'data')), ts),
                         check_vma=False)
```

profile of v0, /device:TPU:81, one launch (start us, length us, event | category | flops | bytes accessed | tf_op | source)
XLA Modules:
  0.0 892.5 jit_solution(10690028462392033459)
XLA Ops:
  7.2 0.0 copy-start
  7.2 0.1 all-gather.4.cloned.1.call-start
  7.3 17.6 %copy.46 = f32[1,4096,1024]{1,2,0:T(8,128)} copy(f32[1,4096,1024]{2,1,0:T(8,128)} %param.15) | data formatting | bytes 33554432 | tf_op args[2]
  24.9 0.0 copy-done
  24.9 8.2 fusion.20
  33.1 2.3 copy-done.2
  35.4 12.2 %fusion.27 = (bf16[256,4096]{1,0:T(8,128)(2,1)S(1)}, f32[256,4096]{1,0:T(8,128)}) fusion(f32[256,1024]{1,0:T(8,128)S(1)} %fusion.20, f32[1,1024,4096]{2,1,0:T(8,128)S(1)} %copy-done.2), kind=kOutput, calls=%fused_computation.55 | convolution fusion | flops 2215903232 | bytes 24117248 | tf_op jit(solution)/shard_map/dot_general | solution.py:63
  47.6 0.0 copy-done.8
  47.6 0.0 copy-done.13
  47.6 8.9 %fusion.99 = f32[256,1024]{1,0:T(8,128)S(1)} fusion(f32[256,1024]{1,0:T(8,128)S(1)} %fusion.20, bf16[256,4096]{1,0:T(8,128)(2,1)S(1)} %get-tuple-element.57, bf16[256,1024]{1,0:T(8,128)(2,1)S(1)} %copy-done.13, f32[1,4096,1024]{1,2,0:T(8,128)} %copy.46), kind=kOutput, calls=%fused_computation.130 | convolution fusion | flops 2148532224 | bytes 21495808 | tf_op jit(solution)/shard_map/dot_general | solution.py:66
  56.6 0.0 copy-done.6
  56.6 0.0 copy-done.9
  56.6 8.0 fusion.24
  64.5 0.0 copy-start.4
  64.5 9.0 %fusion.101 = bf16[256,1024]{1,0:T(8,128)(2,1)S(1)} fusion(f32[256,1024]{1,0:T(8,128)S(1)} %fusion.99, bf16[256,4096]{1,0:T(8,128)(2,1)S(1)} %fusion.24, f32[1,1024,4096]{2,1,0:T(8,128)} %param.14), kind=kOutput, calls=%fused_computation.132 | convolution fusion | flops 2148007936 | bytes 20447232 | tf_op jit(solution)/shard_map/dot_general | solution.py:76
  73.5 0.0 copy-done.4
  73.6 5.8 convolution_convert_fusion.2
  79.4 7.6 copy.68
  86.9 101.1 %all_to_all.27 = bf16[8,512,1024]{1,2,0:T(8,128)(2,1)} all-to-all(bf16[8,512,1024]{1,2,0:T(8,128)(2,1)} %bitcast.152), channel_id=1, replica_groups=mesh['rep'=4,'data'=8] {'data'}, dimensions={0} | all-to-all | bytes 16777216 | tf_op jit(solution)/shard_map/all_to_all | solution.py:33
  188.0 6.0 reduce_sum.100
  194.0 0.1 all-gather.4.cloned.1.call-update
  194.1 0.1 all-gather.6.cloned.1.call-start
  194.2 0.0 copy-done.5
  194.2 3.6 convolution_convert_fusion.1
  197.8 132.0 %all_to_all.28 = bf16[8,128,4096]{2,1,0:T(8,128)(2,1)} all-to-all(bf16[8,128,4096]{2,1,0:T(8,128)(2,1)S(1)} %bitcast.150), channel_id=1, replica_groups=mesh['rep'=4,'data'=8] {'data'}, dimensions={0} | all-to-all | bytes 16777216 | tf_op jit(solution)/shard_map/all_to_all | solution.py:33
  329.8 6.2 reduce_sum.103
  336.0 0.1 all-gather.6.cloned.1.call-update
  336.1 0.2 all-gather.8.cloned.1.call-start
  336.3 0.0 copy-done.7
  336.3 2.4 convolution_convert_fusion
  338.7 132.1 %all_to_all.29 = bf16[8,512,1024]{2,1,0:T(8,128)(2,1)} all-to-all(bf16[8,512,1024]{2,1,0:T(8,128)(2,1)S(1)} %bitcast.149), channel_id=1, replica_groups=mesh['rep'=4,'data'=8] {'data'}, dimensions={0} | all-to-all | bytes 16777216 | tf_op jit(solution)/shard_map/all_to_all | solution.py:33
  470.8 5.7 reduce_sum.106
  476.4 1.4 copy.53
  477.8 0.1 all-gather.8.cloned.1.call-update
  477.8 17.4 %copy.51 = f32[4096,1024]{0,1:T(8,128)} copy(f32[4096,1024]{1,0:T(8,128)} %param.13) | data formatting | bytes 33554432 | tf_op args[0]
  495.3 17.4 %copy.45 = f32[4096,1024]{0,1:T(8,128)} copy(f32[4096,1024]{1,0:T(8,128)} %param.16) | data formatting | bytes 33554432 | tf_op args[3]
  512.7 17.4 %copy.49 = f32[4096,1024]{0,1:T(8,128)} copy(f32[4096,1024]{1,0:T(8,128)} %param.17) | data formatting | bytes 33554432 | tf_op args[4]
  530.1 10.7 %multiply_reduce_fusion.3 = f32[]{:T(128)} fusion(f32[4096,1024]{1,0:T(8,128)} %param.13), kind=kLoop, calls=%fused_computation.29 | loop fusion | flops 8388607 | bytes 16777220 | tf_op jit(solution)/shard_map/reduce_sum | solution.py:27
  541.5 17.5 %copy.52 = f32[1,4096,1024]{1,2,0:T(8,128)} copy(f32[1,4096,1024]{2,1,0:T(8,128)} %param.20) | data formatting | bytes 33554432 | tf_op args[7]
  559.0 17.5 %copy.54 = f32[1,4096,1024]{1,2,0:T(8,128)} copy(f32[1,4096,1024]{2,1,0:T(8,128)} %param.21) | data formatting | bytes 33554432 | tf_op args[8]
  576.5 0.0 copy-done.11
  576.5 1.0 copy.56
  577.6 30.9 %multiply_reduce_fusion.2 = (f32[]{:T(128)}, f32[4096,1024]{0,1:T(8,128)}, f32[4096,1024]{0,1:T(8,128)}) fusion(f32[4096,1024]{0,1:T(8,128)} %copy.51, bf16[4096,1024]{0,1:T(8,128)(2,1)} %all-gather.4.cloned.1.call-done, f32[4096,1024]{0,1:T(8,128)} %copy.45, f32[4096,1024]{0,1:T(8,128)} %copy.49), kind=kLoop, calls=%fused_computation.27 | loop fusion | flops 67108864 | bytes 92274688 | tf_op jit(solution)/shard_map/reduce_sum | solution.py:27
  609.1 0.0 all-gather.6.cloned.1.call-done
  609.2 38.0 %multiply_reduce_fusion.1 = (f32[]{:T(128)}, f32[1024,4096]{1,0:T(8,128)}, f32[1,1024,4096]{2,1,0:T(8,128)}, f32[1,1024,4096]{2,1,0:T(8,128)}, f32[]{:T(128)}) fusion(f32[1,1024,4096]{2,1,0:T(8,128)} %param.14, f32[1,1024,4096]{2,1,0:T(8,128)} %param.19, bf16[1024,4096]{1,0:T(8,128)(2,1)} %all-gather.6.cloned.1.call-done, f32[1,1024,4096]{2,1,0:T(8,128)} %param.18), kind=kLoop, calls=%fused_computation.25 | loop fusion | flops 75497472 | bytes 109051912 | tf_op jit(solution)/shard_map/reduce_sum | solution.py:27
  648.6 17.4 %copy.59 = f32[4096,1024]{1,0:T(8,128)} copy(f32[4096,1024]{0,1:T(8,128)} %get-tuple-element.49) | data formatting | bytes 33554432
  666.0 17.4 %copy.60 = f32[4096,1024]{1,0:T(8,128)} copy(f32[4096,1024]{0,1:T(8,128)} %get-tuple-element.50) | data formatting | bytes 33554432
  683.5 23.7 %multiply_subtract_fusion = f32[4096,1024]{0,1:T(8,128)} fusion(f32[4096,1024]{0,1:T(8,128)} %copy.51, f32[]{:T(128)S(6)} %mul.225, f32[4096,1024]{0,1:T(8,128)} %get-tuple-element.50, f32[4096,1024]{0,1:T(8,128)} %get-tuple-element.49), kind=kLoop, calls=%fused_computation.26 | loop fusion | flops 33554432 | bytes 67108864 | tf_op jit(solution)/shard_map/sub | solution.py:28
  707.1 17.6 %copy.57 = f32[4096,1024]{1,0:T(8,128)} copy(f32[4096,1024]{0,1:T(8,128)} %multiply_subtract_fusion) | data formatting | bytes 33554432
  724.7 0.0 copy-done.10
  724.7 8.1 fusion.87
  732.9 0.0 all-gather.8.cloned.1.call-done
  732.9 38.1 %multiply_reduce_fusion = (f32[]{:T(128)}, f32[4096,1024]{0,1:T(8,128)}, f32[1,4096,1024]{1,2,0:T(8,128)}, f32[1,4096,1024]{1,2,0:T(8,128)}, f32[]{:T(128)}) fusion(f32[1,4096,1024]{1,2,0:T(8,128)} %copy.46, f32[1,4096,1024]{1,2,0:T(8,128)} %copy.54, bf16[4096,1024]{0,1:T(8,128)(2,1)} %all-gather.8.cloned.1.call-done, f32[1,4096,1024]{1,2,0:T(8,128)} %copy.52), kind=kLoop, calls=%fused_computation.24 | loop fusion | flops 75497472 | bytes 109051912 | tf_op jit(solution)/shard_map/reduce_sum | solution.py:27
  772.4 0.0 copy-start.3
  772.4 18.0 %fusion.22 = f32[1,1024,4096]{2,1,0:T(8,128)} fusion(f32[1024,4096]{1,0:T(8,128)} %get-tuple-element.47, f32[]{:T(128)S(6)} %mul.247, f32[1,1024,4096]{2,1,0:T(8,128)} %param.14), kind=kLoop, calls=%fused_computation.46 | loop fusion | flops 8388608 | bytes 50331652 | tf_op jit(solution)/shard_map/stack | solution.py:47
  790.5 3.4 copy-done.3
  793.9 11.8 %fusion.23 = f32[1,4096,1024]{1,2,0:T(8,128)} fusion(f32[4096,1024]{0,1:T(8,128)S(1)} %copy-done.3, f32[]{:T(128)S(6)} %mul.262, f32[1,4096,1024]{1,2,0:T(8,128)} %copy.46), kind=kLoop, calls=%fused_computation.47 | loop fusion | flops 8388608 | bytes 50331652 | tf_op jit(solution)/shard_map/stack | solution.py:47
  805.7 0.0 copy-done.12
  805.7 25.5 %multiply_reduce_fusion.4 = (f32[256]{0:T(256)S(1)}, f32[256,1024]{0,1:T(8,128)S(1)}) fusion(bf16[256,1024]{0,1:T(8,128)(2,1)S(1)} %copy-done.12, f32[256,1024]{0,1:T(8,128)S(1)} %fusion.87, f32[4096,1024]{0,1:T(8,128)} %get-tuple-element.45, f32[]{:T(128)S(6)} %mul.262, f32[1,4096,1024]{1,2,0:T(8,128)} %copy.46, f32[1024,4096]{1,0:T(8,128)} %get-tuple-element.47, ...), kind=kOutput, calls=%fused_computation.133 | convolution fusion | flops 4389863424 | bytes 69731336 | tf_op jit(solution)/shard_map/dot_general | solution.py:42
  831.2 1.3 copy.63
  832.5 0.6 broadcast_multiply_fusion
  833.1 17.4 %copy.58 = f32[1,4096,1024]{2,1,0:T(8,128)} copy(f32[1,4096,1024]{1,2,0:T(8,128)} %fusion.23) | data formatting | bytes 33554432
  850.5 17.4 %copy.61 = f32[1,4096,1024]{2,1,0:T(8,128)} copy(f32[1,4096,1024]{1,2,0:T(8,128)} %get-tuple-element.52) | data formatting | bytes 33554432
  868.0 17.6 %copy.62 = f32[1,4096,1024]{2,1,0:T(8,128)} copy(f32[1,4096,1024]{1,2,0:T(8,128)} %get-tuple-element.51) | data formatting | bytes 33554432
  (13 shorter events, 0.0 us)
Async XLA Ops:
  7.2 17.7 %copy-start = (bf16[256,4096]{1,0:T(8,128)(2,1)S(1)}, bf16[256,4096]{1,0:T(8,128)(2,1)}, u32[]{:S(2)}) copy-start(bf16[256,4096]{1,0:T(8,128)(2,1)} %param.22) | copy-start | bytes 6291460
  7.2 570.3 %all-gather.4.cloned.1.call-start = ((), (), s32[]{:S(2)}) async-start(), calls=%async_computation.3 | async-start | bytes 9437184 | tf_op jit(solution)/shard_map/all_gather | solution.py:35
  24.9 10.5 %copy-start.2 = (f32[1,1024,4096]{2,1,0:T(8,128)S(1)}, f32[1,1024,4096]{2,1,0:T(8,128)}, u32[]{:S(2)}) copy-start(f32[1,1024,4096]{2,1,0:T(8,128)} %param.14) | copy-start | bytes 50331652
  35.4 12.2 %copy-start.8 = (f32[256,1024]{1,0:T(8,128)}, f32[256,1024]{1,0:T(8,128)S(1)}, u32[]{:S(2)}) copy-start(f32[256,1024]{1,0:T(8,128)S(1)} %fusion.20) | copy-start | bytes 3145732
  35.4 12.2 %copy-start.13 = (bf16[256,1024]{1,0:T(8,128)(2,1)S(1)}, bf16[256,1024]{1,0:T(8,128)(2,1)}, u32[]{:S(2)}) copy-start(bf16[256,1024]{1,0:T(8,128)(2,1)} %param.23) | copy-start | bytes 1572868
  47.6 9.0 %copy-start.6 = (bf16[256,4096]{1,0:T(8,128)(2,1)}, bf16[256,4096]{1,0:T(8,128)(2,1)S(1)}, u32[]{:S(2)}) copy-start(bf16[256,4096]{1,0:T(8,128)(2,1)S(1)} %get-tuple-element.57) | copy-start | bytes 6291460
  47.6 9.0 %copy-start.9 = (f32[256,4096]{1,0:T(8,128)S(1)}, f32[256,4096]{1,0:T(8,128)}, u32[]{:S(2)}) copy-start(f32[256,4096]{1,0:T(8,128)} %get-tuple-element.58) | copy-start | bytes 12582916
  64.5 9.0 %copy-start.4 = (bf16[256,4096]{1,0:T(8,128)(2,1)}, bf16[256,4096]{1,0:T(8,128)(2,1)S(1)}, u32[]{:S(2)}) copy-start(bf16[256,4096]{1,0:T(8,128)(2,1)S(1)} %fusion.24) | copy-start | bytes 6291460
  188.0 6.1 copy-start.5
  194.1 415.1 %all-gather.6.cloned.1.call-start = ((), (), s32[]{:S(2)}) async-start(), calls=%async_computation.4 | async-start | bytes 9437184 | tf_op jit(solution)/shard_map/all_gather | solution.py:35
  329.8 6.5 copy-start.7
  336.1 396.8 %all-gather.8.cloned.1.call-start = ((), (), s32[]{:S(2)}) async-start(), calls=%async_computation.5 | async-start | bytes 9437184 | tf_op jit(solution)/shard_map/all_gather | solution.py:35
  559.0 17.5 %copy-start.11 = (bf16[256,1024]{1,0:T(8,128)(2,1)S(1)}, bf16[256,1024]{1,0:T(8,128)(2,1)}, u32[]{:S(2)}) copy-start(bf16[256,1024]{1,0:T(8,128)(2,1)} %param.25) | copy-start | bytes 1572868
  707.1 17.6 %copy-start.10 = (bf16[256,4096]{1,0:T(8,128)(2,1)S(1)}, bf16[256,4096]{1,0:T(8,128)(2,1)}, u32[]{:S(2)}) copy-start(bf16[256,4096]{1,0:T(8,128)(2,1)} %param.24) | copy-start | bytes 6291460
  772.4 21.4 %copy-start.3 = (f32[4096,1024]{0,1:T(8,128)S(1)}, f32[4096,1024]{0,1:T(8,128)}, u32[]{:S(2)}) copy-start(f32[4096,1024]{0,1:T(8,128)} %get-tuple-element.45) | copy-start | bytes 50331652
  793.8 11.9 %copy-start.12 = (bf16[256,1024]{0,1:T(8,128)(2,1)S(1)}, bf16[256,1024]{0,1:T(8,128)(2,1)}, u32[]{:S(2)}) copy-start(bf16[256,1024]{0,1:T(8,128)(2,1)} %copy.56) | copy-start | bytes 1572868
  868.0 17.6 %copy-start.1 = (bf16[256,4096]{1,0:T(8,128)(2,1)S(1)}, bf16[256,4096]{1,0:T(8,128)(2,1)}, u32[]{:S(2)}) copy-start(bf16[256,4096]{1,0:T(8,128)(2,1)} %param.22) | copy-start | bytes 6291460
Sparse Core Ops, SparseCore 0:
  194.2 114.3 all-gather.3
  336.2 115.3 all-gather.5
  478.0 46.6 all-gather.7
where the time goes:
time: 902 us; the launch traced here: 893 us
  blocking collectives  365 us (40%)
  local copies, waits for them, and re-layouts  227 us (25%)
  other arithmetic  190 us (21%)
  matrix products  91.7 us (10%)
  between operations  18.5 us (2%)
    all_to_all x3, blocking collectives, group_sum(): lax.all_to_all(g, 'data', 0, 0, tiled=True).reshape(p, rows // p, cols)  365 us
    unnamed x42, local copies, waits for them, and re-layouts  218 us
    reduce_sum x4, other arithmetic, lamb(): r = jnp.sqrt(jnp.sum(w * w)) / jnp.sqrt(jnp.sum(u * u))  118 us
    another operation x2, other arithmetic, stacked(): return jnp.stack([u[k] for u in ups])  29.9 us
    dot_general x1, matrix products, forward(): h = h + jnp.dot(s, w2b[l], preferred_element_type=F32)  25.5 us
    sub x1, other arithmetic, lamb(): return (w - ETA * r * u, m2, v2)  23.7 us
  transfers between devices with their start and end apart: 3, of which 0 were waited for; matrix products, arithmetic and copies ran while one was open for 30% of the time, Pallas kernels for 0%

commit v1 on v0

v1 whole, which is shorter than its diff:
```python
import functools

import jax
import jax.numpy as jnp
from jax import lax
from jax.experimental import pallas as pl
from jax.experimental.pallas import tpu as pltpu
from jax.sharding import PartitionSpec as P

BETA1 = 0.9
BETA2 = 0.999
BC1 = 1.0 / (1.0 - BETA1 ** 10)
BC2 = 1.0 / (1.0 - BETA2 ** 10)
EPS = 1e-12
WD = 0.01
ETA = 0.05
R2 = 0.7071067811865476
R2PI = 0.3989422804014327
BF = jnp.bfloat16
F32 = jnp.float32


def gelu(a):
    return 0.5 * a * (1.0 + lax.erf(a * R2))


def gelu_grad(a):
    return 0.5 * (1.0 + lax.erf(a * R2)) + a * jnp.exp(-0.5 * a * a) * R2PI


MESH = pl.DeviceIdType.MESH
ROUNDS = 6


def fold8(x):
    return jnp.sum(x.reshape(x.shape[0] // 8, 8, x.shape[1]), axis=0)


def moments(w, g, m, v):
    m2 = BETA1 * m + (1.0 - BETA1) * g
    v2 = BETA2 * v + (1.0 - BETA2) * g * g
    u = BC1 * m2 / (jnp.sqrt(BC2 * v2) + EPS) + WD * w
    return m2, v2, u


def sum_kernel(p, s_ref, gb_ref, hb_ref, a_ref, g_ref, x_ref, w2, m2, v2, w1, m1, v1, wi, mi, vi,
               o2, o1, oi, cs_ref,
               st, pr, pt, rb, e_s, h_t, g0_s, wa, wb, lw, gst, ns, nr,
               d_send, d_recv, r_send, r_recv, credit, pcredit, w_sem, l_sem, o_sem, n_send, n_recv):
    me = lax.axis_index('data')
    core = lax.rem(me, 2)
    chip = lax.div(me, 2)
    nc = p // 2
    partner = me + 1 - 2 * core
    right = lax.rem(me + 2, p)
    left = lax.rem(me + p - 2, p)
    dims_t = (((1,), (1,)), ((), ()))

    def owner(t, k):
        return 2 * lax.rem(chip + t, nc) + k

    def remote(src, dst, ss, rs, dev):
        return pltpu.make_async_remote_copy(src_ref=src, dst_ref=dst, send_sem=ss, recv_sem=rs,
                                            device_id={'data': dev}, device_id_type=MESH)

    def d2d(b, t):
        return remote(st.at[b, t], pr.at[b, t], d_send.at[b, t], d_recv.at[b, t], partner)

    up, lo = pl.ds(0, 128), pl.ds(128, 128)
    routes = ((2, up, 0, right), (2, lo, 1, left), (1, lo, 2, right), (3, up, 3, left), (1, up, 4, right), (3, lo, 5, left))

    def ring(b, n):
        t, half, slot, dev = routes[n]
        return remote(pt.at[b, t, half], rb.at[b, slot], r_send.at[b, n], r_recv.at[b, n], dev)

    def tile(r, j, store):
        h = r % 2
        if r // 2 == 1:
            rows = pl.ds(pl.multiple_of(j * 128 + h * 64, 64), 64)
            for q in range(4):
                d = jnp.dot(h_t[rows, :], e_s[:, q * 1024:(q + 1) * 1024], preferred_element_type=F32)
                store(pl.ds(q * 64, 64), d.astype(BF))
        else:
            x, y = (s_ref, gb_ref) if r < 2 else (x_ref, g0_s)
            cols = pl.ds(pl.multiple_of(j * 512 + h * 256, 256), 256)
            d = jnp.dot(x[:, cols].T, y[...], preferred_element_type=F32)
            store(pl.ds(0, 256), d.astype(BF))

    def s1(r):
        b = r % 2
        if r >= 2:
            pl.semaphore_wait(pcredit, 1)

        def theirs(t, _):
            def put(rows, d):
                st[b, t, rows] = d
            tile(r, owner(t, 1 - core), put)

            @pl.when(t > 0)
            def _():
                d2d(b, t - 1).start()
            return 0

        lax.fori_loop(0, nc, theirs, 0)

        def ours(t, _):
            def put(rows, d):
                pt[b, t, rows] = d.astype(F32)
            tile(r, owner(t, core), put)

            @pl.when(t == 0)
            def _():
                d2d(b, nc - 1).start()
            return 0

        lax.fori_loop(0, nc, ours, 0)

    def s2(r):
        b = r % 2
        if r >= 2:
            pl.semaphore_wait(credit.at[0], 1)
            pl.semaphore_wait(credit.at[1], 1)
        for t in (2, 1, 3, 0):
            d2d(b, t).wait_recv()
            pt[b, t] += pr[b, t].astype(F32)
            if t == 2:
                ring(b, 0).start()
                ring(b, 1).start()
            elif t == 1:
                ring(b, 2).start()
            elif t == 3:
                ring(b, 3).start()
        for t in range(nc):
            d2d(b, t).wait_send()
        if r + 2 < ROUNDS:
            pl.semaphore_signal(pcredit, inc=1, device_id={'data': partner}, device_id_type=MESH)

    def s3(r):
        b = r % 2
        ring(b, 0).wait_recv()
        pt[b, 1, up] += rb[b, 0]
        ring(b, 4).start()
        ring(b, 1).wait_recv()
        pt[b, 3, lo] += rb[b, 1]
        ring(b, 5).start()

    def shard_loads(r):
        k, h = r // 2, r % 2
        out = []
        for n, ref in enumerate(((w2, m2, v2), (w1, m1, v1), (wi, mi, vi))[k]):
            if k == 1:
                for q in range(4):
                    rows = pl.ds(pl.multiple_of(me * 128 + h * 64, 64), 64)
                    out.append(pltpu.make_async_copy(ref.at[rows, pl.ds(q * 1024, 1024)],
                                                     lw.at[n, pl.ds(q * 64, 64)], l_sem.at[n, q]))
            else:
                rows = pl.ds(pl.multiple_of(me * 512 + h * 256, 256), 256)
                out.append(pltpu.make_async_copy(ref.at[rows], lw.at[n], l_sem.at[n, 0]))
        return out

    def put_out(r):
        k, h = r // 2, r % 2
        rows = pl.ds(h * 256, 256)
        return pltpu.make_async_copy(gst.at[k, rows], (o2, o1, oi)[k].at[rows], o_sem.at[k, h])

    def s4(r):
        b, k, h = r % 2, r // 2, r % 2
        loads = shard_loads(r)
        for c in loads:
            c.start()
        for n in (2, 3, 4, 5):
            ring(b, n).wait_recv()
        gst[k, pl.ds(h * 256, 128)] = (pt[b, 0, up] + rb[b, 4] + rb[b, 3]).astype(BF)
        gst[k, pl.ds(h * 256 + 128, 128)] = (pt[b, 0, lo] + rb[b, 5] + rb[b, 2]).astype(BF)
        for n in range(6):
            ring(b, n).wait_send()
        if r + 2 < ROUNDS:
            pl.semaphore_signal(credit.at[0], inc=1, device_id={'data': right}, device_id_type=MESH)
            pl.semaphore_signal(credit.at[1], inc=1, device_id={'data': left}, device_id_type=MESH)
        for c in loads:
            c.wait()
        put_out(r).start()
        sw = jnp.zeros((8, 1024), F32)
        su = jnp.zeros((8, 1024), F32)
        for i in range(4):
            rows = pl.ds(i * 64, 64)
            w = lw[0, rows]
            _, _, u = moments(w, gst[k, pl.ds(h * 256 + i * 64, 64)].astype(F32), lw[1, rows], lw[2, rows])
            sw += fold8(w * w)
            su += fold8(u * u)
        for n, t in enumerate((sw, su)):
            f = t[:, 0:128]
            for q in range(1, 8):
                f += t[:, q * 128:(q + 1) * 128]
            row = pl.ds((2 * k + n) * 8, 8)
            if h == 0:
                ns[row] = f
            else:
                ns[row] += f

    def load_a(i):
        return pltpu.make_async_copy(w2.at[pl.ds(i * 256, 256)], wa.at[lax.rem(i, 2)], w_sem.at[lax.rem(i, 2)])

    def load_b(i):
        return pltpu.make_async_copy(w1.at[pl.ds(i * 128, 128)], wb.at[lax.rem(i, 2)], w_sem.at[lax.rem(i, 2)])

    def make_e():
        n = s_ref.shape[1] // 256
        load_a(0).start()
        h_t[...] = hb_ref[...].T

        def body(i, _):
            @pl.when(i + 1 < n)
            def _():
                load_a(i + 1).start()
            load_a(i).wait()
            cols = pl.ds(pl.multiple_of(i * 256, 256), 256)
            d = lax.dot_general(gb_ref[...], wa[lax.rem(i, 2)].astype(BF), dims_t, preferred_element_type=F32)
            e_s[:, cols] = (d * gelu_grad(a_ref[:, cols])).astype(BF)
            return 0

        lax.fori_loop(0, n, body, 0)

    def make_g0():
        n = gb_ref.shape[1] // 128
        load_b(0).start()

        def body(i, _):
            @pl.when(i + 1 < n)
            def _():
                load_b(i + 1).start()
            load_b(i).wait()
            cols = pl.ds(pl.multiple_of(i * 128, 128), 128)
            d = lax.dot_general(e_s[...], wb[lax.rem(i, 2)].astype(BF), dims_t, preferred_element_type=F32)
            g0_s[:, cols] = (g_ref[:, cols] + d).astype(BF)
            return 0

        lax.fori_loop(0, n, body, 0)

    barrier = pltpu.get_barrier_semaphore()
    for o in range(1, p):
        pl.semaphore_signal(barrier, inc=1, device_id={'data': lax.rem(me + o, p)}, device_id_type=MESH)
    pl.semaphore_wait(barrier, p - 1)

    s1(0)
    s2(0)
    for r in range(ROUNDS):
        if r + 1 < ROUNDS:
            s1(r + 1)
        s3(r)
        if r + 1 < ROUNDS:
            s2(r + 1)
        if r == 0:
            make_e()
        if r == 2:
            make_g0()
        s4(r)

    def norm(o):
        return remote(ns, nr.at[me], n_send.at[o - 1], n_recv.at[o - 1], lax.rem(me + o, p))

    nr[me] = ns[...]
    for o in range(1, p):
        norm(o).start()
    for o in range(1, p):
        norm(o).wait()
    tot = nr[0]
    for o in range(1, p):
        tot = tot + nr[o]
    for k in range(3):
        nw = jnp.sqrt(jnp.sum(tot[16 * k:16 * k + 8], keepdims=True))
        nu = jnp.sqrt(jnp.sum(tot[16 * k + 8:16 * k + 16], keepdims=True))
        cs_ref[k] = jnp.broadcast_to(ETA * (nw / nu), (8, 128))
    for r in range(ROUNDS):
        put_out(r).wait()


def reduce_grads(p, s, gb, hb, a, g, x, w2, m2, v2, w1, m1, v1, wi, mi, vi):
    vm = pl.BlockSpec(memory_space=pltpu.VMEM)
    hbm = pl.BlockSpec(memory_space=pl.ANY)
    dma, reg = pltpu.SemaphoreType.DMA, pltpu.SemaphoreType.REGULAR
    o = jax.ShapeDtypeStruct((512, 1024), BF)
    tok = x.shape[0]
    return pl.pallas_call(
        functools.partial(sum_kernel, p),
        name='sum_grads',
        in_specs=[vm] * 6 + [hbm] * 9,
        out_specs=[hbm] * 3 + [vm],
        out_shape=[o, o, o, jax.ShapeDtypeStruct((3, 8, 128), F32)],
        scratch_shapes=[
            pltpu.VMEM((2, 4, 256, 1024), BF), pltpu.VMEM((2, 4, 256, 1024), BF), pltpu.VMEM((2, 4, 256, 1024), F32),
            pltpu.VMEM((2, 6, 128, 1024), F32), pltpu.VMEM((tok, 4096), BF), pltpu.VMEM((1024, tok), BF),
            pltpu.VMEM((tok, 1024), BF), pltpu.VMEM((2, 256, 1024), F32), pltpu.VMEM((2, 128, 4096), F32),
            pltpu.VMEM((3, 256, 1024), F32), pltpu.VMEM((3, 512, 1024), BF), pltpu.VMEM((48, 128), F32), pltpu.VMEM((p, 48, 128), F32),
            dma((2, 4)), dma((2, 4)), dma((2, 6)), dma((2, 6)), reg((2,)), reg, dma((2,)), dma((3, 4)), dma((3, 2)),
            dma((p - 1,)), dma((p - 1,)),
        ],
        compiler_params=pltpu.CompilerParams(collective_id=0, has_side_effects=True, vmem_limit_bytes=60 * 2 ** 20),
        cost_estimate=pl.CostEstimate(flops=10 ** 11, bytes_accessed=10 ** 8, transcendentals=0),
    )(s, gb, hb, a, g, x, w2, m2, v2, w1, m1, v1, wi, mi, vi)


def lamb_kernel(kind, *refs):
    w_ref, m_ref, v_ref, g_ref, c_ref, x_ref = refs[:6]
    h_ref = refs[6] if kind == 'out' else None
    wo_ref, mo_ref, vo_ref, o_ref = refs[-4:]
    w = w_ref[...]
    g = g_ref[...].reshape(w.shape).astype(F32)
    m2, v2, u = moments(w, g, m_ref[...], v_ref[...])
    mo_ref[...] = m2
    vo_ref[...] = v2
    wn = w - c_ref[0:1, 0:1] * u
    wo_ref[...] = wn
    d = jnp.dot(x_ref[...], wn.astype(BF), preferred_element_type=F32)
    if kind == 'cols':
        o_ref[...] = gelu(d).astype(BF)
    else:
        j = pl.program_id(0)

        @pl.when(j == 0)
        def _():
            o_ref[...] = d if kind == 'in' else h_ref[...] + d

        @pl.when(j > 0)
        def _():
            o_ref[...] += d


def lamb(kind, w, m, v, g, c, x, h=None):
    rows, cols = w.shape
    tok = x.shape[0]
    whole = lambda s: pl.BlockSpec(s, lambda i: (0,) * len(s))
    if kind == 'cols':
        nb = cols // 256
        blk = pl.BlockSpec((rows, 256), lambda i: (0, i))
        q = g.shape[-1] // 256
        g_spec = pl.BlockSpec(g.shape[:2] + (None, g.shape[3], 256), lambda i: (0, 0, i // q, 0, i % q))
        x_spec = whole((tok, rows))
        o_spec = pl.BlockSpec((tok, 256), lambda i: (0, i))
        o_shape = jax.ShapeDtypeStruct((tok, cols), BF)
    else:
        nb = rows // 256
        blk = pl.BlockSpec((256, cols), lambda i: (i, 0))
        g_spec = blk
        x_spec = pl.BlockSpec((tok, 256), lambda i: (0, i))
        o_spec = whole((tok, cols))
        o_shape = jax.ShapeDtypeStruct((tok, cols), F32)
    ins = [w, m, v, g, c, x]
    specs = [blk] * 3 + [g_spec, whole((8, 128)), x_spec]
    if h is not None:
        ins.append(h)
        specs.append(whole((tok, cols)))
    f = jax.ShapeDtypeStruct((rows, cols), F32)
    return pl.pallas_call(
        functools.partial(lamb_kernel, kind),
        name='lamb_' + kind,
        grid=(nb,),
        in_specs=specs,
        out_specs=[blk, blk, blk, o_spec],
        out_shape=[f, f, f, o_shape],
        compiler_params=pltpu.CompilerParams(dimension_semantics=('arbitrary',), vmem_limit_bytes=40 * 2 ** 20),
        cost_estimate=pl.CostEstimate(flops=30 * 10 ** 9, bytes_accessed=rows * cols * 26, transcendentals=0),
    )(*ins)


def solution(mesh):
    p = mesh.shape['data']

    def gather(s):
        return lax.all_gather(s, 'data', axis=0, tiled=True)

    def step(wi, w1, w2, mi, vi, m1, v1, m2, v2, x0, y0, x1, y1):
        w1, w2, m1, v1, m2, v2 = (t[0] for t in (w1, w2, m1, v1, m2, v2))
        d = wi.shape[1]
        scale = 1.0 / (x0.shape[0] * p * d)
        h = jnp.dot(x0, wi.astype(BF), preferred_element_type=F32)
        hb = h.astype(BF)
        a = jnp.dot(hb, w1.astype(BF), preferred_element_type=F32)
        s = gelu(a).astype(BF)
        h = h + jnp.dot(s, w2.astype(BF), preferred_element_type=F32)
        g = (h - y0.astype(F32)) * scale
        s2, s1, si, c = reduce_grads(p, s, g.astype(BF), hb, a, g, x0, w2, m2, v2, w1, m1, v1, wi, mi, vi)
        gi = gather(si)
        g1 = gather(s1).reshape(p, 2, 4, 64, 1024)
        g2 = gather(s2)
        wi_n, mi_n, vi_n, h = lamb('in', wi, mi, vi, gi, c[2], x1)
        w1_n, m1_n, v1_n, s = lamb('cols', w1, m1, v1, g1, c[1], h.astype(BF))
        w2_n, m2_n, v2_n, h = lamb('out', w2, m2, v2, g2, c[0], s, h)
        loss = jnp.sum((h - y1.astype(F32)) ** 2, axis=-1) / (2.0 * d)
        return (wi_n, w1_n[None], w2_n[None], mi_n, vi_n, m1_n[None], v1_n[None], m2_n[None], v2_n[None], loss, h)

    w2s = P('rep', None)
    w3s = P('rep', None, None)
    ts = P(('rep', 'data'), None)
    return jax.shard_map(step, mesh=mesh,
                         in_specs=(w2s, w3s, w3s, w2s, w2s, w3s, w3s, w3s, w3s, ts, ts, ts, ts),
                         out_specs=(w2s, w3s, w3s, w2s, w2s, w3s, w3s, w3s, w3s, P(('rep', 'data')), ts),
                         check_vma=False)
```

time: 902 us -> 460 us (0.51); the launches traced: 893 us -> 460 us
  blocking collectives: 365 us -> 0 us
  Pallas kernels: 0 us -> 351 us
  local copies, waits for them, and re-layouts: 227 us -> 17.8 us
  other arithmetic: 190 us -> 2.08 us
  matrix products: 91.7 us -> 23.4 us
  waiting for transfers between devices: 0.21 us -> 51 us
    all_to_all x3 -> x0, blocking collectives: 365 us -> none  [group_sum(): lax.all_to_all(g, 'data', 0, 0, tiled=True).reshape(p, rows // p, cols)]
    pallas_call x0 -> x4, Pallas kernels: none -> 351 us  [the longest x1 225 us: reduce_grads(): pl.pallas_call(functools.partial(sum_kernel, p), name='sum_grads', in_spe...]
    unnamed x42 -> x22, local copies, waits for them, and re-layouts: 218 us -> 17.1 us
    reduce_sum x7 -> x1, other arithmetic: 136 us -> 1.44 us  [step(): loss = jnp.sum((h - y1.astype(F32)) ** 2, axis=-1) / (2.0 * d)]
    dot_general x10 -> x3, matrix products: 91.7 us -> 23.4 us  [the longest x1 10 us: step(): h = h + jnp.dot(s, w2.astype(BF), preferred_element_type=F32)]
    all_gather x3, waiting for transfers between devices: 0.04 us -> 49.5 us  [gather(): return lax.all_gather(s, 'data', axis=0, tiled=True)]
    another operation x2 -> x0, other arithmetic: 29.9 us -> none  [stacked(): return jnp.stack([u[k] for u in ups])]
    sub x1 -> x0, other arithmetic: 23.7 us -> none  [lamb(): return (w - ETA * r * u, m2, v2)]
  transfers between devices with their start and end apart: 3 -> 3, of which waited for: 0 -> 3; matrix products, arithmetic and copies ran while one was open for 30% -> 0% of each run, Pallas kernels for 0% -> 18%
where the time goes in v1:
time: 460 us
  Pallas kernels  351 us (76%)
  waiting for transfers between devices  51 us (11%)
  matrix products  23.4 us (5%)
  local copies, waits for them, and re-layouts  17.8 us (4%)
  between operations  13.9 us (3%)
    pallas_call x1, Pallas kernels, reduce_grads(): pl.pallas_call(functools.partial(sum_kernel, p), name='sum_grads', in_spe...  225 us
    pallas_call x3, Pallas kernels, lamb(): pl.pallas_call(functools.partial(lamb_kernel, kind), name='lamb_' + kind,...  127 us
    all_gather x3, waiting for transfers between devices, gather(): return lax.all_gather(s, 'data', axis=0, tiled=True)  49.5 us
    unnamed x22, local copies, waits for them, and re-layouts  17.1 us
    dot_general x1, matrix products, step(): h = h + jnp.dot(s, w2.astype(BF), preferred_element_type=F32)  10 us
  transfers between devices with their start and end apart: 3, of which 3 were waited for; matrix products, arithmetic and copies ran while one was open for 0% of the time, Pallas kernels for 18%

profile of v1, /device:TPU:81, one launch (start us, length us, event | category | flops | bytes accessed | tf_op | source)
XLA Modules:
  0.0 459.6 jit_solution(10198104028007803276)
XLA Ops:
  7.2 0.1 all-gather.4.cloned.1.call-start
  7.3 0.0 copy-start.6
  7.3 8.9 %fusion.19 = (bf16[256,1024]{1,0:T(8,128)(2,1)S(1)}, f32[256,1024]{1,0:T(8,128)S(1)}) fusion(bf16[256,4096]{1,0:T(8,128)(2,1)} %x_ref.1, f32[4096,1024]{1,0:T(8,128)} %refs_0_.1), kind=kOutput, calls=%fused_computation.17 | convolution fusion | flops 2151940096 | bytes 20447232 | tf_op jit(solution)/shard_map/dot_general | solution.py:376
  16.2 0.0 copy-start.8
  16.2 0.0 copy-start.9
  16.2 2.4 copy-done.6
  18.6 4.4 multiply_convert_fusion
  23.1 0.0 copy-start.7
  23.1 0.0 copy-done.9
  23.1 10.0 %fusion.20 = (bf16[256,1024]{1,0:T(8,128)(2,1)}, f32[256,1024]{1,0:T(8,128)}) fusion(bf16[256,1024]{1,0:T(8,128)(2,1)S(1)} %copy-done.9, f32[256,1024]{1,0:T(8,128)S(1)} %get-tuple-element.47, bf16[256,4096]{1,0:T(8,128)(2,1)S(1)} %get-tuple-element.48.s_ref, f32[1,4096,1024]{2,1,0:T(8,128)} %param.15), kind=kOutput, calls=%fused_computation.18 | convolution fusion | flops 2148794368 | bytes 22020096 | tf_op jit(solution)/shard_map/dot_general | solution.py:380
  33.1 0.0 copy-done.8
  33.1 0.0 copy-done.7
  33.1 224.5 %sum_grads.1 = (bf16[512,1024]{1,0:T(8,128)(2,1)}, bf16[512,1024]{1,0:T(8,128)(2,1)}, bf16[512,1024]{1,0:T(8,128)(2,1)}, f32[3,8,128]{2,1,0:T(8,128)}) custom-call(bf16[256,4096]{1,0:T(8,128)(2,1)} %copy-done.7, bf16[256,1024]{1,0:T(8,128)(2,1)} %get-tuple-element.50.gb_ref, bf16[256,1024]{1,0:T(8,128)(2,1)} %copy-done.8, ...), custom_call_target="tpu_custom_call" | custom-call | flops 99999997952 | bytes 100000000 | tf_op jit(solution)/shard_map/sum_grads/pallas_call | solution.py:284
  257.6 0.1 all-gather.4.cloned.1.call-update
  257.7 0.1 all-gather.6.cloned.1.call-start
  257.8 0.7 all-gather.6.cloned.1.call-update
  258.5 0.1 all-gather.8.cloned.1.call-start
  258.6 0.7 all-gather.8.cloned.1.call-update
  259.3 0.7 slice_bitcast_fusion
  260.0 46.1 %all-gather.4.cloned.1.call-done.refs_3_ = bf16[4096,1024]{1,0:T(8,128)(2,1)} async-done(((bf16[512,1024]{1,0:T(8,128)(2,1)}), bf16[4096,1024]{1,0:T(8,128)(2,1)}) %all-gather.4.cloned.1.call-update) | async-done | bytes 8388624 | tf_op jit(solution)/shard_map/all_gather | solution.py:370
  306.1 0.0 copy-start.2
  306.1 3.4 copy-done.2
  309.5 0.0 copy-start.3
  309.5 1.6 copy-done.3
  311.1 43.2 %lamb_in.1 = (f32[4096,1024]{1,0:T(8,128)}, f32[4096,1024]{1,0:T(8,128)}, f32[4096,1024]{1,0:T(8,128)}, f32[256,1024]{1,0:T(8,128)S(1)}) custom-call(f32[4096,1024]{1,0:T(8,128)} %refs_0_.1, f32[4096,1024]{1,0:T(8,128)} %refs_1_.1, f32[4096,1024]{1,0:T(8,128)} %refs_2_.1, bf16[4096,1024]{1,0:T(8,128)(2,1)S(1)} %copy-done.2, ...), custom_call_target="tpu_custom_call" | custom-call | flops 30000001024 | bytes 109051904 | tf_op jit(solution)/shard_map/lamb_in/pallas_call | solution.py:354
  354.3 0.1 convert_element_type.34.refs_5_
  354.4 0.1 all-gather.6.cloned.1.call-done
  354.5 0.0 copy-start.1
  354.5 3.4 copy-done.1
  357.9 40.4 %lamb_cols.1 = (f32[1024,4096]{1,0:T(8,128)}, f32[1024,4096]{1,0:T(8,128)}, f32[1024,4096]{1,0:T(8,128)}, bf16[256,4096]{1,0:T(8,128)(2,1)S(1)}) custom-call(f32[1024,4096]{1,0:T(8,128)} %bitcast.50, f32[1024,4096]{1,0:T(8,128)} %bitcast.54, f32[1024,4096]{1,0:T(8,128)} %bitcast.56, bf16[8,2,4,64,1024]{4,3,2,1,0:T(8,128)(2,1)S(1)} %bitcast.48, ...), custom_call_target="tpu_custom_call" | custom-call | flops 30000001024 | bytes 109051904 | tf_op jit(solution)/shard_map/lamb_cols/pallas_call | solution.py:354
  398.3 0.0 copy-start.4
  398.3 1.3 copy-done.4
  399.6 3.2 all-gather.8.cloned.1.call-done.refs_3_
  402.9 0.0 copy-start
  402.9 3.4 copy-done
  406.3 0.0 copy-start.5
  406.3 1.6 copy-done.5
  407.9 0.0 copy-start.10
  407.9 43.1 %lamb_out.1 = (f32[4096,1024]{1,0:T(8,128)}, f32[4096,1024]{1,0:T(8,128)}, f32[4096,1024]{1,0:T(8,128)}, f32[256,1024]{1,0:T(8,128)}) custom-call(f32[4096,1024]{1,0:T(8,128)} %bitcast.52, f32[4096,1024]{1,0:T(8,128)} %bitcast.58, f32[4096,1024]{1,0:T(8,128)} %bitcast.60, bf16[4096,1024]{1,0:T(8,128)(2,1)S(1)} %copy-done, ...), custom_call_target="tpu_custom_call" | custom-call | flops 30000001024 | bytes 109051904 | tf_op jit(solution)/shard_map/lamb_out/pallas_call | solution.py:354
  451.0 0.0 copy-done.10
  451.0 1.4 multiply_reduce_fusion
  452.5 0.6 broadcast_multiply_fusion
Async XLA Ops:
  7.2 298.9 %all-gather.4.cloned.1.call-start = ((), (), s32[]{:S(2)}) async-start(), calls=%async_computation | async-start | bytes 9437184 | tf_op jit(solution)/shard_map/all_gather | solution.py:370
  7.3 11.4 %copy-start.6 = (f32[1,1024,4096]{2,1,0:T(8,128)S(1)}, f32[1,1024,4096]{2,1,0:T(8,128)}, u32[]{:S(2)}) copy-start(f32[1,1024,4096]{2,1,0:T(8,128)} %param.14) | copy-start | bytes 50331652
  16.2 17.0 %copy-start.8 = (bf16[256,1024]{1,0:T(8,128)(2,1)}, bf16[256,1024]{1,0:T(8,128)(2,1)S(1)}, u32[]{:S(2)}) copy-start(bf16[256,1024]{1,0:T(8,128)(2,1)S(1)} %get-tuple-element.46.hb_ref) | copy-start | bytes 1572868
  16.2 6.9 %copy-start.9 = (bf16[256,1024]{1,0:T(8,128)(2,1)S(1)}, bf16[256,1024]{1,0:T(8,128)(2,1)}, u32[]{:S(2)}) copy-start(bf16[256,1024]{1,0:T(8,128)(2,1)} %param.23) | copy-start | bytes 1572868
  23.1 10.1 %copy-start.7 = (bf16[256,4096]{1,0:T(8,128)(2,1)}, bf16[256,4096]{1,0:T(8,128)(2,1)S(1)}, u32[]{:S(2)}) copy-start(bf16[256,4096]{1,0:T(8,128)(2,1)S(1)} %get-tuple-element.48.s_ref) | copy-start | bytes 6291460
  257.7 96.8 %all-gather.6.cloned.1.call-start = ((), (), s32[]{:S(2)}) async-start(), calls=%async_computation.1 | async-start | bytes 9437184 | tf_op jit(solution)/shard_map/all_gather | solution.py:370
  258.5 144.4 %all-gather.8.cloned.1.call-start = ((), (), s32[]{:S(2)}) async-start(), calls=%async_computation.2 | async-start | bytes 9437184 | tf_op jit(solution)/shard_map/all_gather | solution.py:370
  306.1 3.4 copy-start.2
  309.5 1.6 copy-start.3
  354.5 3.4 copy-start.1
  398.3 1.3 copy-start.4
  402.9 3.4 copy-start
  406.3 1.6 copy-start.5
  407.9 43.2 %copy-start.10 = (bf16[256,1024]{1,0:T(8,128)(2,1)S(1)}, bf16[256,1024]{1,0:T(8,128)(2,1)}, u32[]{:S(2)}) copy-start(bf16[256,1024]{1,0:T(8,128)(2,1)} %param.25) | copy-start | bytes 1572868
Sparse Core Ops, SparseCore 0:
  257.8 48.2 all-gather.3
  307.8 46.6 all-gather.5
  356.1 46.6 all-gather.7

commit v2 on v1

--- a/solution.py
+++ b/solution.py
@@ -43,10 +43,10 @@
     return m2, v2, u
 
 
-def sum_kernel(p, s_ref, gb_ref, hb_ref, a_ref, g_ref, x_ref, w2, m2, v2, w1, m1, v1, wi, mi, vi,
+def sum_kernel(p, x_ref, y_ref, w2, m2, v2, w1, m1, v1, wi, mi, vi,
                o2, o1, oi, cs_ref,
-               st, pr, pt, rb, e_s, h_t, g0_s, wa, wb, lw, gst, ns, nr,
-               d_send, d_recv, r_send, r_recv, credit, pcredit, w_sem, l_sem, o_sem, n_send, n_recv):
+               s_ref, gb_ref, hb_ref, a_ref, g_ref, st, pr, pt, rb, e_s, h_t, g0_s, wa, wb, lw, gst, ns, nr,
+               d_send, d_recv, r_send, r_recv, credit, pcredit, w_sem, l_sem, o_sem, n_send, n_recv, a_send, a_recv, b_send, b_recv, f_sem):
     me = lax.axis_index('data')
     core = lax.rem(me, 2)
     chip = lax.div(me, 2)
@@ -75,42 +75,46 @@
 
     def tile(r, j, store):
         h = r % 2
-        if r // 2 == 1:
-            rows = pl.ds(pl.multiple_of(j * 128 + h * 64, 64), 64)
+        if r // 2 == 2:
+            cols = pl.ds(pl.multiple_of(j * 512 + h * 256, 256), 256)
             for q in range(4):
-                d = jnp.dot(h_t[rows, :], e_s[:, q * 1024:(q + 1) * 1024], preferred_element_type=F32)
-                store(pl.ds(q * 64, 64), d.astype(BF))
+                d = jnp.dot(h_t[q * 256:(q + 1) * 256, :], e_s[:, cols], preferred_element_type=F32)
+                store(pl.ds(q * 256, 256), d.astype(BF))
         else:
             x, y = (s_ref, gb_ref) if r < 2 else (x_ref, g0_s)
             cols = pl.ds(pl.multiple_of(j * 512 + h * 256, 256), 256)
             d = jnp.dot(x[:, cols].T, y[...], preferred_element_type=F32)
-            store(pl.ds(0, 256), d.astype(BF))
+            store(pl.ds(0, 1024), d.astype(BF))
 
     def s1(r):
         b = r % 2
         if r >= 2:
             pl.semaphore_wait(pcredit, 1)
 
-        def theirs(t, _):
-            def put(rows, d):
-                st[b, t, rows] = d
+        def theirs(i, _):
+            t = lax.rem(i + 2, nc)
+
+            def put(cols, d):
+                st[b, t, :, cols] = d
             tile(r, owner(t, 1 - core), put)
 
-            @pl.when(t > 0)
-            def _():
-                d2d(b, t - 1).start()
+            @pl.when(i > 0)
+            def _():
+                d2d(b, lax.rem(i + 1, nc)).start()
             return 0
 
         lax.fori_loop(0, nc, theirs, 0)
 
-        def ours(t, _):
-            def put(rows, d):
-                pt[b, t, rows] = d.astype(F32)
+        def ours(i, _):
+            t = lax.rem(i + 2, nc)
+
+            def put(cols, d):
+                pt[b, t, :, cols] = d.astype(F32)
             tile(r, owner(t, core), put)
 
-            @pl.when(t == 0)
-            def _():
-                d2d(b, nc - 1).start()
+            @pl.when(i == 0)
+            def _():
+                d2d(b, 1).start()
             return 0
 
         lax.fori_loop(0, nc, ours, 0)
@@ -120,7 +124,7 @@
         if r >= 2:
             pl.semaphore_wait(credit.at[0], 1)
             pl.semaphore_wait(credit.at[1], 1)
-        for t in (2, 1, 3, 0):
+        for t in (2, 3, 1, 0):
             d2d(b, t).wait_recv()
             pt[b, t] += pr[b, t].astype(F32)
             if t == 2:
@@ -147,21 +151,58 @@
     def shard_loads(r):
         k, h = r // 2, r % 2
         out = []
-        for n, ref in enumerate(((w2, m2, v2), (w1, m1, v1), (wi, mi, vi))[k]):
-            if k == 1:
+        at = pl.ds(pl.multiple_of(me * 512 + h * 256, 256), 256)
+        for n, ref in enumerate(((w2, m2, v2), (wi, mi, vi), (w1, m1, v1))[k]):
+            if k == 2:
                 for q in range(4):
-                    rows = pl.ds(pl.multiple_of(me * 128 + h * 64, 64), 64)
-                    out.append(pltpu.make_async_copy(ref.at[rows, pl.ds(q * 1024, 1024)],
-                                                     lw.at[n, pl.ds(q * 64, 64)], l_sem.at[n, q]))
+                    part = pl.ds(q * 256, 256)
+                    out.append(pltpu.make_async_copy(ref.at[part, at], lw.at[n, :, part], l_sem.at[n, q]))
             else:
-                rows = pl.ds(pl.multiple_of(me * 512 + h * 256, 256), 256)
-                out.append(pltpu.make_async_copy(ref.at[rows], lw.at[n], l_sem.at[n, 0]))
+                out.append(pltpu.make_async_copy(ref.at[at], lw.at[n], l_sem.at[n, 0]))
         return out
 
     def put_out(r):
         k, h = r // 2, r % 2
         rows = pl.ds(h * 256, 256)
-        return pltpu.make_async_copy(gst.at[k, rows], (o2, o1, oi)[k].at[rows], o_sem.at[k, h])
+        dst = oi.at[block(me, h)] if k == 1 else (o2, oi, o1)[k].at[rows]
+        return pltpu.make_async_copy(gst.at[k, rows], dst, o_sem.at[k, h])
+
+    def block(j, h):
+        return pl.ds(pl.multiple_of(j * 512 + h * 256, 256), 256)
+
+    def ag(n):
+        h = n % 2
+        if n < 4:
+            src, j, dev = gst.at[1, pl.ds(h * 256, 256)], me, (right, left)[n // 2]
+        else:
+            j, dev = (left, right)[h], (right, left)[h]
+            src = oi.at[block(j, h)]
+        return remote(src, oi.at[block(j, h)], a_send.at[n], a_recv.at[n], dev)
+
+    def ag_pair(n):
+        h = n % 2
+        j = (me, left, right, lax.rem(me + 4, p))[n // 2]
+        src = gst.at[1, pl.ds(h * 256, 256)] if n < 2 else oi.at[block(j, h)]
+        return remote(src, oi.at[block(j, h)], b_send.at[n], b_recv.at[n], partner)
+
+    def ag_own(h):
+        ag(h).start()
+        ag(2 + h).start()
+        ag_pair(h).start()
+
+    def ag_near(h):
+        ag(h).wait_recv()
+        if h == 0:
+            ag(4).start()
+        ag(2 + h).wait_recv()
+        if h == 1:
+            ag(5).start()
+        ag_pair(2 + h).start()
+        ag_pair(4 + h).start()
+
+    def ag_far(h):
+        ag(4 + h).wait_recv()
+        ag_pair(6 + h).start()
 
     def s4(r):
         b, k, h = r % 2, r // 2, r % 2
@@ -237,9 +278,96 @@
 
         lax.fori_loop(0, n, body, 0)
 
+    def f_buf(u):
+        return pt.at[lax.div(u, 2), pl.ds(2 * lax.rem(u, 2), 2)]
+
+    def f_copy(src, u, n):
+        return pltpu.make_async_copy(src, pt.at[lax.div(u, 2), 2 * lax.rem(u, 2) + n], f_sem.at[u, n])
+
+    def f_start(i):
+        u = lax.rem(i, 4)
+        k, o = lax.div(i, 8), lax.rem(i, 8)
+        for n in range(2):
+            rows = pl.ds(pl.multiple_of(o * 512 + n * 256, 256), 256)
+
+            @pl.when(k == 0)
+            def _():
+                f_copy(wi.at[rows], u, n).start()
+
+            @pl.when(k == 1)
+            def _():
+                part = pl.ds(pl.multiple_of(lax.rem(o, 2) * 512 + n * 256, 256), 256)
+                f_copy(w1.at[part, pl.ds(pl.multiple_of(lax.div(o, 2) * 1024, 1024), 1024)], u, n).start()
+
+            @pl.when(k == 2)
+            def _():
+                f_copy(w2.at[rows], u, n).start()
+
+    def f_take(i):
+        u = lax.rem(i, 4)
+        for n in range(2):
+            f_copy(wi.at[pl.ds(0, 256)], u, n).wait()
+        return f_buf(u)[...].reshape(512, 1024).astype(BF)
+
+    def f_loop(k, body):
+        def one(n, _):
+            i = 8 * k + n
+            body(n, f_take(i))
+
+            @pl.when(i + 4 < 24)
+            def _():
+                f_start(i + 4)
+            return 0
+
+        lax.fori_loop(0, 8, one, 0)
+
+    def chunk(n):
+        return pl.ds(pl.multiple_of(n * 512, 512), 512)
+
+    def f_in(n, w):
+        d = jnp.dot(x_ref[:, chunk(n)], w, preferred_element_type=F32)
+
+        @pl.when(n == 0)
+        def _():
+            g_ref[...] = d
+
+        @pl.when(n > 0)
+        def _():
+            g_ref[...] += d
+
+    def f_mid(n, w):
+        cols = pl.ds(pl.multiple_of(lax.div(n, 2) * 1024, 1024), 1024)
+
+        @pl.when(lax.rem(n, 2) == 0)
+        def _():
+            a_ref[:, cols] = jnp.dot(hb_ref[:, 0:512], w, preferred_element_type=F32)
+
+        @pl.when(lax.rem(n, 2) == 1)
+        def _():
+            a_ref[:, cols] += jnp.dot(hb_ref[:, 512:1024], w, preferred_element_type=F32)
+
+            def act(q, _):
+                part = pl.ds(pl.multiple_of(lax.div(n, 2) * 1024 + q * 256, 256), 256)
+                s_ref[:, part] = gelu(a_ref[:, part]).astype(BF)
+                return 0
+
+            lax.fori_loop(0, 4, act, 0)
+
+    def f_out(n, w):
+        g_ref[...] += jnp.dot(s_ref[:, chunk(n)], w, preferred_element_type=F32)
+
     barrier = pltpu.get_barrier_semaphore()
     for o in range(1, p):
         pl.semaphore_signal(barrier, inc=1, device_id={'data': lax.rem(me + o, p)}, device_id_type=MESH)
+    for i in range(4):
+        f_start(jnp.int32(i))
+    f_loop(0, f_in)
+    hb_ref[...] = g_ref[...].astype(BF)
+    f_loop(1, f_mid)
+    f_loop(2, f_out)
+    scale = 1.0 / (x_ref.shape[0] * p * g_ref.shape[1])
+    g_ref[...] = (g_ref[...] - y_ref[...].astype(F32)) * scale
+    gb_ref[...] = g_ref[...].astype(BF)
     pl.semaphore_wait(barrier, p - 1)
 
     s1(0)
@@ -252,9 +380,17 @@
             s2(r + 1)
         if r == 0:
             make_e()
-        if r == 2:
             make_g0()
+        if r == 3:
+            ag_near(0)
+        if r == 4:
+            ag_near(1)
+            ag_far(0)
+        if r == 5:
+            ag_far(1)
         s4(r)
+        if r // 2 == 1:
+            ag_own(r % 2)
 
     def norm(o):
         return remote(ns, nr.at[me], n_send.at[o - 1], n_recv.at[o - 1], lax.rem(me + o, p))
@@ -273,93 +409,144 @@
         cs_ref[k] = jnp.broadcast_to(ETA * (nw / nu), (8, 128))
     for r in range(ROUNDS):
         put_out(r).wait()
-
-
-def reduce_grads(p, s, gb, hb, a, g, x, w2, m2, v2, w1, m1, v1, wi, mi, vi):
+    for n in range(6):
+        ag(n).wait_send()
+    for n in range(8):
+        ag_pair(n).wait()
+
+
+def reduce_grads(p, x, y, w2, m2, v2, w1, m1, v1, wi, mi, vi):
     vm = pl.BlockSpec(memory_space=pltpu.VMEM)
-    hbm = pl.BlockSpec(memory_space=pl.ANY)
+    hbm = pl.BlockSpec(memory_space=pltpu.HBM)
     dma, reg = pltpu.SemaphoreType.DMA, pltpu.SemaphoreType.REGULAR
     o = jax.ShapeDtypeStruct((512, 1024), BF)
     tok = x.shape[0]
     return pl.pallas_call(
         functools.partial(sum_kernel, p),
         name='sum_grads',
-        in_specs=[vm] * 6 + [hbm] * 9,
+        in_specs=[vm] * 2 + [hbm] * 9,
         out_specs=[hbm] * 3 + [vm],
-        out_shape=[o, o, o, jax.ShapeDtypeStruct((3, 8, 128), F32)],
+        out_shape=[o, o, jax.ShapeDtypeStruct((512 * p, 1024), BF), jax.ShapeDtypeStruct((3, 8, 128), F32)],
         scratch_shapes=[
+            pltpu.VMEM((tok, 4096), BF), pltpu.VMEM((tok, 1024), BF), pltpu.VMEM((tok, 1024), BF),
+            pltpu.VMEM((tok, 4096), F32), pltpu.VMEM((tok, 1024), F32),
             pltpu.VMEM((2, 4, 256, 1024), BF), pltpu.VMEM((2, 4, 256, 1024), BF), pltpu.VMEM((2, 4, 256, 1024), F32),
             pltpu.VMEM((2, 6, 128, 1024), F32), pltpu.VMEM((tok, 4096), BF), pltpu.VMEM((1024, tok), BF),
             pltpu.VMEM((tok, 1024), BF), pltpu.VMEM((2, 256, 1024), F32), pltpu.VMEM((2, 128, 4096), F32),
             pltpu.VMEM((3, 256, 1024), F32), pltpu.VMEM((3, 512, 1024), BF), pltpu.VMEM((48, 128), F32), pltpu.VMEM((p, 48, 128), F32),
             dma((2, 4)), dma((2, 4)), dma((2, 6)), dma((2, 6)), reg((2,)), reg, dma((2,)), dma((3, 4)), dma((3, 2)),
-            dma((p - 1,)), dma((p - 1,)),
+            dma((p - 1,)), dma((p - 1,)), dma((6,)), dma((6,)), dma((8,)), dma((8,)), dma((4, 2)),
         ],
         compiler_params=pltpu.CompilerParams(collective_id=0, has_side_effects=True, vmem_limit_bytes=60 * 2 ** 20),
         cost_estimate=pl.CostEstimate(flops=10 ** 11, bytes_accessed=10 ** 8, transcendentals=0),
-    )(s, gb, hb, a, g, x, w2, m2, v2, w1, m1, v1, wi, mi, vi)
-
-
-def lamb_kernel(kind, *refs):
-    w_ref, m_ref, v_ref, g_ref, c_ref, x_ref = refs[:6]
-    h_ref = refs[6] if kind == 'out' else None
-    wo_ref, mo_ref, vo_ref, o_ref = refs[-4:]
-    w = w_ref[...]
-    g = g_ref[...].reshape(w.shape).astype(F32)
-    m2, v2, u = moments(w, g, m_ref[...], v_ref[...])
-    mo_ref[...] = m2
-    vo_ref[...] = v2
-    wn = w - c_ref[0:1, 0:1] * u
-    wo_ref[...] = wn
-    d = jnp.dot(x_ref[...], wn.astype(BF), preferred_element_type=F32)
-    if kind == 'cols':
-        o_ref[...] = gelu(d).astype(BF)
-    else:
-        j = pl.program_id(0)
-
-        @pl.when(j == 0)
+    )(x, y, w2, m2, v2, w1, m1, v1, wi, mi, vi)
+
+
+def lamb_kernel(kind, nb, has_h, w, m, v, g, c_ref, x_ref, *refs):
+    h_ref = refs[0] if has_h else None
+    wo, mo, vo, o_ref, ib, gb, ob, i_sem, o_sem = refs[has_h:]
+    nbuf = ib.shape[0]
+    size = gb.shape[1] if kind != 'cols' else ib.shape[3]
+
+    def at(i):
+        s = pl.ds(pl.multiple_of(i * size, size), size)
+        return (slice(None), s) if kind == 'cols' else (s, slice(None))
+
+    def loads(i):
+        b = lax.rem(i, nbuf)
+        rows = pl.ds(pl.multiple_of(i * gb.shape[1], gb.shape[1]), gb.shape[1])
+        return [pltpu.make_async_copy(r.at[at(i)], ib.at[b, n], i_sem.at[b, n]) for n, r in enumerate((w, m, v))] + [
+            pltpu.make_async_copy(g.at[rows], gb.at[b], i_sem.at[b, 3])]
+
+    def stores(i):
+        b = lax.rem(i, nbuf)
+        return [pltpu.make_async_copy(ob.at[b, n], r.at[at(i)], o_sem.at[b, n]) for n, r in enumerate((wo, mo, vo))]
+
+    for i in range(nbuf):
+        for t in loads(i):
+            t.start()
+    c = c_ref[0:1, 0:1]
+
+    def block(i, _):
+        b = lax.rem(i, nbuf)
+        for t in loads(i):
+            t.wait()
+
+        @pl.when(i >= nbuf)
         def _():
-            o_ref[...] = d if kind == 'in' else h_ref[...] + d
-
-        @pl.when(j > 0)
+            for t in stores(i - nbuf):
+                t.wait()
+
+        def update(grows, gcols, rows, cols):
+            w_t = ib[b, 0, rows, cols]
+            m2, v2, u = moments(w_t, gb[b, grows, gcols].astype(F32), ib[b, 1, rows, cols], ib[b, 2, rows, cols])
+            ob[b, 0, rows, cols] = w_t - c * u
+            ob[b, 1, rows, cols] = m2
+            ob[b, 2, rows, cols] = v2
+
+        def part(n, _):
+            for q in range(4):
+                lanes = pl.ds(q * 256, 256)
+                if kind == 'cols':
+                    off = pl.multiple_of(n * 64, 64)
+                    update(pl.ds(off, 64), lanes, pl.ds(q * 256 + off, 64), slice(None))
+                else:
+                    rows = pl.ds(pl.multiple_of(n * 64, 64), 64)
+                    update(rows, lanes, rows, lanes)
+            return 0
+
+        lax.fori_loop(0, gb.shape[1] // 64, part, 0)
+        for t in stores(i):
+            t.start()
+
+        @pl.when(i + nbuf < nb)
         def _():
-            o_ref[...] += d
-
-
-def lamb(kind, w, m, v, g, c, x, h=None):
+            for t in loads(i + nbuf):
+                t.start()
+
+        x = x_ref[...] if kind == 'cols' else x_ref[:, at(i)[0]]
+        d = jnp.dot(x, ob[b, 0].astype(BF), preferred_element_type=F32)
+        if kind == 'cols':
+            o_ref[:, at(i)[1]] = gelu(d).astype(BF)
+        else:
+            @pl.when(i == 0)
+            def _():
+                o_ref[...] = h_ref[...] + d if has_h else d
+
+            @pl.when(i > 0)
+            def _():
+                o_ref[...] += d
+        return 0
+
+    lax.fori_loop(0, nb, block, 0)
+    for i in range(nb - nbuf, nb):
+        for t in stores(i):
+            t.wait()
+
+
+def lamb(kind, w, m, v, g, c, x, h=None, size=256, nbuf=4):
     rows, cols = w.shape
     tok = x.shape[0]
-    whole = lambda s: pl.BlockSpec(s, lambda i: (0,) * len(s))
+    hbm = pl.BlockSpec(memory_space=pltpu.HBM)
+    vm = pl.BlockSpec(memory_space=pltpu.VMEM)
     if kind == 'cols':
-        nb = cols // 256
-        blk = pl.BlockSpec((rows, 256), lambda i: (0, i))
-        q = g.shape[-1] // 256
-        g_spec = pl.BlockSpec(g.shape[:2] + (None, g.shape[3], 256), lambda i: (0, 0, i // q, 0, i % q))
-        x_spec = whole((tok, rows))
-        o_spec = pl.BlockSpec((tok, 256), lambda i: (0, i))
+        nb, blk, gblk = cols // size, (rows, size), (256, 1024)
         o_shape = jax.ShapeDtypeStruct((tok, cols), BF)
     else:
-        nb = rows // 256
-        blk = pl.BlockSpec((256, cols), lambda i: (i, 0))
-        g_spec = blk
-        x_spec = pl.BlockSpec((tok, 256), lambda i: (0, i))
-        o_spec = whole((tok, cols))
+        nb, blk, gblk = rows // size, (size, cols), (size, cols)
         o_shape = jax.ShapeDtypeStruct((tok, cols), F32)
-    ins = [w, m, v, g, c, x]
-    specs = [blk] * 3 + [g_spec, whole((8, 128)), x_spec]
-    if h is not None:
-        ins.append(h)
-        specs.append(whole((tok, cols)))
+    ins = [w, m, v, g, c, x] + ([] if h is None else [h])
     f = jax.ShapeDtypeStruct((rows, cols), F32)
     return pl.pallas_call(
-        functools.partial(lamb_kernel, kind),
+        functools.partial(lamb_kernel, kind, nb, int(h is not None)),
         name='lamb_' + kind,
-        grid=(nb,),
-        in_specs=specs,
-        out_specs=[blk, blk, blk, o_spec],
+        in_specs=[hbm] * 4 + [vm] * (len(ins) - 4),
+        out_specs=[hbm] * 3 + [vm],
         out_shape=[f, f, f, o_shape],
-        compiler_params=pltpu.CompilerParams(dimension_semantics=('arbitrary',), vmem_limit_bytes=40 * 2 ** 20),
-        cost_estimate=pl.CostEstimate(flops=30 * 10 ** 9, bytes_accessed=rows * cols * 26, transcendentals=0),
+        scratch_shapes=[pltpu.VMEM((nbuf, 3) + blk, F32), pltpu.VMEM((nbuf,) + gblk, BF), pltpu.VMEM((nbuf, 3) + blk, F32),
+                        pltpu.SemaphoreType.DMA((nbuf, 4)), pltpu.SemaphoreType.DMA((nbuf, 3))],
+        compiler_params=pltpu.CompilerParams(vmem_limit_bytes=52 * 2 ** 20),
+        cost_estimate=pl.CostEstimate(flops=40 * 10 ** 9, bytes_accessed=rows * cols * 26, transcendentals=0),
     )(*ins)
 
 
@@ -372,19 +559,11 @@
     def step(wi, w1, w2, mi, vi, m1, v1, m2, v2, x0, y0, x1, y1):
         w1, w2, m1, v1, m2, v2 = (t[0] for t in (w1, w2, m1, v1, m2, v2))
         d = wi.shape[1]
-        scale = 1.0 / (x0.shape[0] * p * d)
-        h = jnp.dot(x0, wi.astype(BF), preferred_element_type=F32)
-        hb = h.astype(BF)
-        a = jnp.dot(hb, w1.astype(BF), preferred_element_type=F32)
-        s = gelu(a).astype(BF)
-        h = h + jnp.dot(s, w2.astype(BF), preferred_element_type=F32)
-        g = (h - y0.astype(F32)) * scale
-        s2, s1, si, c = reduce_grads(p, s, g.astype(BF), hb, a, g, x0, w2, m2, v2, w1, m1, v1, wi, mi, vi)
-        gi = gather(si)
-        g1 = gather(s1).reshape(p, 2, 4, 64, 1024)
+        s2, s1, gi, c = reduce_grads(p, x0, y0, w2, m2, v2, w1, m1, v1, wi, mi, vi)
+        g1 = gather(s1)
         g2 = gather(s2)
-        wi_n, mi_n, vi_n, h = lamb('in', wi, mi, vi, gi, c[2], x1)
-        w1_n, m1_n, v1_n, s = lamb('cols', w1, m1, v1, g1, c[1], h.astype(BF))
+        wi_n, mi_n, vi_n, h = lamb('in', wi, mi, vi, gi, c[1], x1)
+        w1_n, m1_n, v1_n, s = lamb('cols', w1, m1, v1, g1, c[2], h.astype(BF))
         w2_n, m2_n, v2_n, h = lamb('out', w2, m2, v2, g2, c[0], s, h)
         loss = jnp.sum((h - y1.astype(F32)) ** 2, axis=-1) / (2.0 * d)
         return (wi_n, w1_n[None], w2_n[None], mi_n, vi_n, m1_n[None], v1_n[None], m2_n[None], v2_n[None], loss, h)

time: 460 us -> 423 us (0.920)
  Pallas kernels: 351 us -> 388 us
  waiting for transfers between devices: 51 us -> 17.6 us
  matrix products: 23.4 us -> 0 us
  local copies, waits for them, and re-layouts: 17.8 us -> 0.7 us
    pallas_call x1, Pallas kernels: 225 us -> 270 us  [reduce_grads(): pl.pallas_call(functools.partial(sum_kernel, p), name='sum_grads', in_spe...]
    all_gather x3 -> x2, waiting for transfers between devices: 49.5 us -> 16.9 us  [gather(): return lax.all_gather(s, 'data', axis=0, tiled=True)]
    dot_general x3 -> x0, matrix products: 23.4 us -> none  [the longest x1 10 us: step(): h = h + jnp.dot(s, w2.astype(BF), preferred_element_type=F32)]
    unnamed x22 -> x2, local copies, waits for them, and re-layouts: 17.1 us -> 0.01 us
    pallas_call x3, Pallas kernels: 127 us -> 118 us  [lamb(): pl.pallas_call(functools.partial(lamb_kernel, kind, nb, int(h is not None...]
  transfers between devices with their start and end apart: 3 -> 2, of which waited for: 3 -> 2; matrix products, arithmetic and copies ran while one was open for 0% -> 0% of each run, Pallas kernels for 18% -> 19%
where the time goes in v2:
time: 423 us
  Pallas kernels  388 us (92%)
  waiting for transfers between devices  17.6 us (4%)
  between operations  14.1 us (3%)
    pallas_call x1, Pallas kernels, reduce_grads(): pl.pallas_call(functools.partial(sum_kernel, p), name='sum_grads', in_spe...  270 us
    pallas_call x3, Pallas kernels, lamb(): pl.pallas_call(functools.partial(lamb_kernel, kind, nb, int(h is not None...  118 us
    all_gather x2, waiting for transfers between devices, gather(): return lax.all_gather(s, 'data', axis=0, tiled=True)  16.9 us
  transfers between devices with their start and end apart: 2, of which 2 were waited for; matrix products, arithmetic and copies ran while one was open for 0% of the time, Pallas kernels for 19%

profile of v2, /device:TPU:81, one launch (start us, length us, event | category | flops | bytes accessed | tf_op | source)
XLA Modules:
  0.0 422.7 jit_solution(6182217702060184246)
XLA Ops:
  7.2 0.1 all-gather.3.cloned.1.call-start
  7.3 269.8 %sum_grads.1 = (bf16[512,1024]{1,0:T(8,128)(2,1)}, bf16[512,1024]{1,0:T(8,128)(2,1)}, bf16[4096,1024]{1,0:T(8,128)(2,1)}, f32[3,8,128]{2,1,0:T(8,128)}) custom-call(bf16[256,4096]{1,0:T(8,128)(2,1)} %x_ref.2, bf16[256,1024]{1,0:T(8,128)(2,1)} %y_ref.1, f32[4096,1024]{1,0:T(8,128)} %bitcast.24, f32[4096,1024]{1,0:T(8,128)} %bitcast.26, ...), custom_call_target="tpu_custom_call" | custom-call | flops 99999997952 | bytes 100000000 | tf_op jit(solution)/shard_map/sum_grads/pallas_call | solution.py:424
  277.1 0.1 all-gather.3.cloned.1.call-update
  277.2 0.1 all-gather.5.cloned.1.call-start
  277.2 0.7 all-gather.5.cloned.1.call-update
  278.0 0.7 slice_bitcast_fusion
  278.7 39.3 %lamb_in.1 = (f32[4096,1024]{1,0:T(8,128)}, f32[4096,1024]{1,0:T(8,128)}, f32[4096,1024]{1,0:T(8,128)}, f32[256,1024]{1,0:T(8,128)S(1)}) custom-call(f32[4096,1024]{1,0:T(8,128)} %w.1, f32[4096,1024]{1,0:T(8,128)} %m.1, f32[4096,1024]{1,0:T(8,128)} %v.1, bf16[4096,1024]{1,0:T(8,128)(2,1)} %get-tuple-element.27.g, f32[8,128]{1,0:T(8,128)S(1)} %get-tuple-element.45.c_ref, ...), custom_call_target="tpu_custom_call" | custom-call | flops 40000000000 | bytes 109051904 | tf_op jit(solution)/shard_map/lamb_in/pallas_call | solution.py:540
  317.9 0.1 convert_element_type.6.x_ref
  318.0 8.1 %all-gather.3.cloned.1.call-done.g = bf16[4096,1024]{1,0:T(8,128)(2,1)} async-done(((bf16[512,1024]{1,0:T(8,128)(2,1)}), bf16[4096,1024]{1,0:T(8,128)(2,1)}) %all-gather.3.cloned.1.call-update) | async-done | bytes 8388624 | tf_op jit(solution)/shard_map/all_gather | solution.py:557
  326.2 39.7 %lamb_cols.1 = (f32[1024,4096]{1,0:T(8,128)}, f32[1024,4096]{1,0:T(8,128)}, f32[1024,4096]{1,0:T(8,128)}, bf16[256,4096]{1,0:T(8,128)(2,1)}) custom-call(f32[1024,4096]{1,0:T(8,128)} %bitcast.19, f32[1024,4096]{1,0:T(8,128)} %bitcast.21, f32[1024,4096]{1,0:T(8,128)} %bitcast.23, bf16[4096,1024]{1,0:T(8,128)(2,1)} %all-gather.3.cloned.1.call-done.g, ...), custom_call_target="tpu_custom_call" | custom-call | flops 40000000000 | bytes 109051904 | tf_op jit(solution)/shard_map/lamb_cols/pallas_call | solution.py:540
  365.8 8.7 %all-gather.5.cloned.1.call-done.g = bf16[4096,1024]{1,0:T(8,128)(2,1)} async-done(((bf16[512,1024]{1,0:T(8,128)(2,1)}), bf16[4096,1024]{1,0:T(8,128)(2,1)}) %all-gather.5.cloned.1.call-update) | async-done | bytes 8388624 | tf_op jit(solution)/shard_map/all_gather | solution.py:557
  374.5 0.0 copy-start
  374.5 39.3 %lamb_out.1 = (f32[4096,1024]{1,0:T(8,128)}, f32[4096,1024]{1,0:T(8,128)}, f32[4096,1024]{1,0:T(8,128)}, f32[256,1024]{1,0:T(8,128)}) custom-call(f32[4096,1024]{1,0:T(8,128)} %bitcast.25, f32[4096,1024]{1,0:T(8,128)} %bitcast.27, f32[4096,1024]{1,0:T(8,128)} %bitcast.29, bf16[4096,1024]{1,0:T(8,128)(2,1)} %all-gather.5.cloned.1.call-done.g, ...), custom_call_target="tpu_custom_call" | custom-call | flops 40000000000 | bytes 109051904 | tf_op jit(solution)/shard_map/lamb_out/pallas_call | solution.py:540
  413.8 0.0 copy-done
  413.8 1.4 multiply_reduce_fusion
  415.3 0.6 broadcast_multiply_fusion
Async XLA Ops:
  7.2 319.0 %all-gather.3.cloned.1.call-start = ((), (), s32[]{:S(2)}) async-start(), calls=%async_computation | async-start | bytes 9437184 | tf_op jit(solution)/shard_map/all_gather | solution.py:557
  277.2 97.4 %all-gather.5.cloned.1.call-start = ((), (), s32[]{:S(2)}) async-start(), calls=%async_computation.1 | async-start | bytes 9437184 | tf_op jit(solution)/shard_map/all_gather | solution.py:557
  374.5 39.3 %copy-start = (bf16[256,1024]{1,0:T(8,128)(2,1)S(1)}, bf16[256,1024]{1,0:T(8,128)(2,1)}, u32[]{:S(2)}) copy-start(bf16[256,1024]{1,0:T(8,128)(2,1)} %param.25) | copy-start | bytes 1572868
Sparse Core Ops, SparseCore 0:
  277.3 48.8 all-gather.2
  327.8 46.7 all-gather.4

commit v3 on v2

--- a/solution.py
+++ b/solution.py
@@ -44,9 +44,9 @@
 
 
 def sum_kernel(p, x_ref, y_ref, w2, m2, v2, w1, m1, v1, wi, mi, vi,
-               o2, o1, oi, cs_ref,
+               o2, o1, oi, p2, p1, cs_ref,
                s_ref, gb_ref, hb_ref, a_ref, g_ref, st, pr, pt, rb, e_s, h_t, g0_s, wa, wb, lw, gst, ns, nr,
-               d_send, d_recv, r_send, r_recv, credit, pcredit, w_sem, l_sem, o_sem, n_send, n_recv, a_send, a_recv, b_send, b_recv, f_sem):
+               d_send, d_recv, r_send, r_recv, credit, pcredit, w_sem, l_sem, o_sem, n_send, n_recv, a_send, a_recv, b_send, b_recv, f_sem, c_send, c_recv):
     me = lax.axis_index('data')
     core = lax.rem(me, 2)
     chip = lax.div(me, 2)
@@ -91,33 +91,25 @@
         if r >= 2:
             pl.semaphore_wait(pcredit, 1)
 
-        def theirs(i, _):
-            t = lax.rem(i + 2, nc)
-
-            def put(cols, d):
-                st[b, t, :, cols] = d
-            tile(r, owner(t, 1 - core), put)
-
-            @pl.when(i > 0)
-            def _():
-                d2d(b, lax.rem(i + 1, nc)).start()
+        def pair(i, _):
+            s1_pair(r, i)
             return 0
 
-        lax.fori_loop(0, nc, theirs, 0)
-
-        def ours(i, _):
-            t = lax.rem(i + 2, nc)
-
-            def put(cols, d):
-                pt[b, t, :, cols] = d.astype(F32)
-            tile(r, owner(t, core), put)
-
-            @pl.when(i == 0)
-            def _():
-                d2d(b, 1).start()
-            return 0
-
-        lax.fori_loop(0, nc, ours, 0)
+        lax.fori_loop(0, nc, pair, 0)
+
+    def s1_pair(r, i):
+        b = r % 2
+        t = lax.rem(i + 2, nc)
+
+        def theirs(cols, d):
+            st[b, t, :, cols] = d
+
+        def ours(cols, d):
+            pt[b, t, :, cols] = d.astype(F32)
+
+        tile(r, owner(t, 1 - core), theirs)
+        tile(r, owner(t, core), ours)
+        d2d(b, t).start()
 
     def s2(r):
         b = r % 2
@@ -125,19 +117,18 @@
             pl.semaphore_wait(credit.at[0], 1)
             pl.semaphore_wait(credit.at[1], 1)
         for t in (2, 3, 1, 0):
-            d2d(b, t).wait_recv()
-            pt[b, t] += pr[b, t].astype(F32)
-            if t == 2:
-                ring(b, 0).start()
-                ring(b, 1).start()
-            elif t == 1:
-                ring(b, 2).start()
-            elif t == 3:
-                ring(b, 3).start()
+            s2_add(r, t)
         for t in range(nc):
             d2d(b, t).wait_send()
         if r + 2 < ROUNDS:
             pl.semaphore_signal(pcredit, inc=1, device_id={'data': partner}, device_id_type=MESH)
+
+    def s2_add(r, t):
+        b = r % 2
+        d2d(b, t).wait_recv()
+        pt[b, t] += pr[b, t].astype(F32)
+        for n in ((), (2,), (0, 1), (3,))[t]:
+            ring(b, n).start()
 
     def s3(r):
         b = r % 2
@@ -166,6 +157,10 @@
         rows = pl.ds(h * 256, 256)
         dst = oi.at[block(me, h)] if k == 1 else (o2, oi, o1)[k].at[rows]
         return pltpu.make_async_copy(gst.at[k, rows], dst, o_sem.at[k, h])
+
+    def give(k, h):
+        rows = pl.ds(h * 256, 256)
+        return remote(gst.at[k, rows], (p2, None, p1)[k].at[rows], c_send.at[k // 2, h], c_recv.at[k // 2, h], partner)
 
     def block(j, h):
         return pl.ds(pl.multiple_of(j * 512 + h * 256, 256), 256)
@@ -370,8 +365,17 @@
     gb_ref[...] = g_ref[...].astype(BF)
     pl.semaphore_wait(barrier, p - 1)
 
-    s1(0)
-    s2(0)
+    s1_pair(0, jnp.int32(0))
+    s1_pair(0, jnp.int32(1))
+    s2_add(0, 2)
+    s1_pair(0, jnp.int32(2))
+    s2_add(0, 3)
+    s1_pair(0, jnp.int32(3))
+    s2_add(0, 1)
+    s2_add(0, 0)
+    for t in range(nc):
+        d2d(0, t).wait_send()
+    pl.semaphore_signal(pcredit, inc=1, device_id={'data': partner}, device_id_type=MESH)
     for r in range(ROUNDS):
         if r + 1 < ROUNDS:
             s1(r + 1)
@@ -391,6 +395,8 @@
         s4(r)
         if r // 2 == 1:
             ag_own(r % 2)
+        else:
+            give(r // 2, r % 2).start()
 
     def norm(o):
         return remote(ns, nr.at[me], n_send.at[o - 1], n_recv.at[o - 1], lax.rem(me + o, p))
@@ -413,6 +419,8 @@
         ag(n).wait_send()
     for n in range(8):
         ag_pair(n).wait()
+    for n in range(4):
+        give(n // 2 * 2, n % 2).wait()
 
 
 def reduce_grads(p, x, y, w2, m2, v2, w1, m1, v1, wi, mi, vi):
@@ -425,8 +433,8 @@
         functools.partial(sum_kernel, p),
         name='sum_grads',
         in_specs=[vm] * 2 + [hbm] * 9,
-        out_specs=[hbm] * 3 + [vm],
-        out_shape=[o, o, jax.ShapeDtypeStruct((512 * p, 1024), BF), jax.ShapeDtypeStruct((3, 8, 128), F32)],
+        out_specs=[hbm] * 5 + [vm],
+        out_shape=[o, o, jax.ShapeDtypeStruct((512 * p, 1024), BF), o, o, jax.ShapeDtypeStruct((3, 8, 128), F32)],
         scratch_shapes=[
             pltpu.VMEM((tok, 4096), BF), pltpu.VMEM((tok, 1024), BF), pltpu.VMEM((tok, 1024), BF),
             pltpu.VMEM((tok, 4096), F32), pltpu.VMEM((tok, 1024), F32),
@@ -435,74 +443,103 @@
             pltpu.VMEM((tok, 1024), BF), pltpu.VMEM((2, 256, 1024), F32), pltpu.VMEM((2, 128, 4096), F32),
             pltpu.VMEM((3, 256, 1024), F32), pltpu.VMEM((3, 512, 1024), BF), pltpu.VMEM((48, 128), F32), pltpu.VMEM((p, 48, 128), F32),
             dma((2, 4)), dma((2, 4)), dma((2, 6)), dma((2, 6)), reg((2,)), reg, dma((2,)), dma((3, 4)), dma((3, 2)),
-            dma((p - 1,)), dma((p - 1,)), dma((6,)), dma((6,)), dma((8,)), dma((8,)), dma((4, 2)),
+            dma((p - 1,)), dma((p - 1,)), dma((6,)), dma((6,)), dma((8,)), dma((8,)), dma((4, 2)), dma((2, 2)), dma((2, 2)),
         ],
         compiler_params=pltpu.CompilerParams(collective_id=0, has_side_effects=True, vmem_limit_bytes=60 * 2 ** 20),
         cost_estimate=pl.CostEstimate(flops=10 ** 11, bytes_accessed=10 ** 8, transcendentals=0),
     )(x, y, w2, m2, v2, w1, m1, v1, wi, mi, vi)
 
 
-def lamb_kernel(kind, nb, has_h, w, m, v, g, c_ref, x_ref, *refs):
+def lamb_kernel(kind, part, p, nb, size, n_g, has_h, has_y, w, m, v, *refs):
+    g_refs, refs = refs[:n_g], refs[n_g:]
+    c_ref, x_ref, refs = refs[0], refs[1], refs[2:]
     h_ref = refs[0] if has_h else None
-    wo, mo, vo, o_ref, ib, gb, ob, i_sem, o_sem = refs[has_h:]
+    y_ref = refs[has_h] if has_y else None
+    l_ref, refs = (refs[-6], refs[:-6] + refs[-5:]) if has_y else (None, refs)
+    wo, mo, vo, o_ref, ib, gb, ob, i_sem, o_sem = refs[-9:]
     nbuf = ib.shape[0]
-    size = gb.shape[1] if kind != 'cols' else ib.shape[3]
+    grows = gb.shape[1]
+    me = lax.axis_index('data')
+    core = lax.rem(me, 2)
+
+    def which(i):
+        if part == 'all':
+            return i
+        h = lax.rem(i, 2)
+        if part == 'near':
+            return 2 * (me + lax.div(i, 2) * (1 - 2 * core)) + h
+        chip = lax.rem(lax.div(me, 2) + 1 + lax.div(i, 4), p // 2)
+        return 4 * chip + lax.rem(i, 4)
 
     def at(i):
-        s = pl.ds(pl.multiple_of(i * size, size), size)
+        s = pl.ds(pl.multiple_of(which(i) * size, size), size)
         return (slice(None), s) if kind == 'cols' else (s, slice(None))
 
     def loads(i):
         b = lax.rem(i, nbuf)
-        rows = pl.ds(pl.multiple_of(i * gb.shape[1], gb.shape[1]), gb.shape[1])
-        return [pltpu.make_async_copy(r.at[at(i)], ib.at[b, n], i_sem.at[b, n]) for n, r in enumerate((w, m, v))] + [
-            pltpu.make_async_copy(g.at[rows], gb.at[b], i_sem.at[b, 3])]
+        return [pltpu.make_async_copy(r.at[at(i)], ib.at[b, n], i_sem.at[b, n]) for n, r in enumerate((w, m, v))]
+
+    def load_g(i, ref, j):
+        b = lax.rem(i, nbuf)
+        rows = pl.ds(pl.multiple_of(j * grows, grows), grows)
+        return pltpu.make_async_copy(ref.at[rows], gb.at[b], i_sem.at[b, 3])
+
+    def start(i):
+        for t in loads(i):
+            t.start()
+        if part != 'near':
+            load_g(i, g_refs[0], which(i)).start()
+        else:
+            for n in range(2):
+                @pl.when(lax.div(i, 2) == n)
+                def _():
+                    load_g(i, g_refs[n], lax.rem(i, 2)).start()
 
     def stores(i):
         b = lax.rem(i, nbuf)
         return [pltpu.make_async_copy(ob.at[b, n], r.at[at(i)], o_sem.at[b, n]) for n, r in enumerate((wo, mo, vo))]
 
     for i in range(nbuf):
-        for t in loads(i):
-            t.start()
+        start(jnp.int32(i))
     c = c_ref[0:1, 0:1]
+    if kind == 'cols' and has_h:
+        o_ref[...] = h_ref[...]
 
     def block(i, _):
         b = lax.rem(i, nbuf)
         for t in loads(i):
             t.wait()
+        load_g(i, g_refs[0], 0).wait()
 
         @pl.when(i >= nbuf)
         def _():
             for t in stores(i - nbuf):
                 t.wait()
 
-        def update(grows, gcols, rows, cols):
+        def update(grow, gcol, rows, cols):
             w_t = ib[b, 0, rows, cols]
-            m2, v2, u = moments(w_t, gb[b, grows, gcols].astype(F32), ib[b, 1, rows, cols], ib[b, 2, rows, cols])
+            m2, v2, u = moments(w_t, gb[b, grow, gcol].astype(F32), ib[b, 1, rows, cols], ib[b, 2, rows, cols])
             ob[b, 0, rows, cols] = w_t - c * u
             ob[b, 1, rows, cols] = m2
             ob[b, 2, rows, cols] = v2
 
-        def part(n, _):
+        def piece(n, _):
             for q in range(4):
                 lanes = pl.ds(q * 256, 256)
+                off = pl.multiple_of(n * 64, 64)
                 if kind == 'cols':
-                    off = pl.multiple_of(n * 64, 64)
                     update(pl.ds(off, 64), lanes, pl.ds(q * 256 + off, 64), slice(None))
                 else:
-                    rows = pl.ds(pl.multiple_of(n * 64, 64), 64)
-                    update(rows, lanes, rows, lanes)
+                    update(pl.ds(off, 64), lanes, pl.ds(off, 64), lanes)
             return 0
 
-        lax.fori_loop(0, gb.shape[1] // 64, part, 0)
+        lax.fori_loop(0, grows // 64, piece, 0)
         for t in stores(i):
             t.start()
 
         @pl.when(i + nbuf < nb)
         def _():
-            for t in loads(i + nbuf):
-                t.start()
+            start(i + nbuf)
 
         x = x_ref[...] if kind == 'cols' else x_ref[:, at(i)[0]]
         d = jnp.dot(x, ob[b, 0].astype(BF), preferred_element_type=F32)
@@ -519,12 +556,16 @@
         return 0
 
     lax.fori_loop(0, nb, block, 0)
+    if has_y:
+        e = o_ref[...] - y_ref[...].astype(F32)
+        row = jnp.sum(e * e, axis=-1, keepdims=True) / (2.0 * e.shape[1])
+        l_ref[...] = jnp.broadcast_to(row, (e.shape[0], 128)).T[0:8]
     for i in range(nb - nbuf, nb):
         for t in stores(i):
             t.wait()
 
 
-def lamb(kind, w, m, v, g, c, x, h=None, size=256, nbuf=4):
+def lamb(kind, part, p, w, m, v, g, c, x, h=None, y=None, prev=None, size=256, nbuf=4):
     rows, cols = w.shape
     tok = x.shape[0]
     hbm = pl.BlockSpec(memory_space=pltpu.HBM)
@@ -535,18 +576,27 @@
     else:
         nb, blk, gblk = rows // size, (size, cols), (size, cols)
         o_shape = jax.ShapeDtypeStruct((tok, cols), F32)
-    ins = [w, m, v, g, c, x] + ([] if h is None else [h])
+    nb = {'all': nb, 'near': nb // (p // 2), 'far': nb - nb // (p // 2)}[part]
+    ins = [w, m, v, *g, c, x] + [t for t in (h, y) if t is not None]
+    specs = [hbm] * (3 + len(g)) + [vm] * (len(ins) - 3 - len(g))
+    alias = {}
+    for k, t in enumerate(prev or ()):
+        alias[len(ins)] = k
+        ins.append(t)
+        specs.append(hbm)
     f = jax.ShapeDtypeStruct((rows, cols), F32)
+    loss = [] if y is None else [jax.ShapeDtypeStruct((8, tok), F32)]
     return pl.pallas_call(
-        functools.partial(lamb_kernel, kind, nb, int(h is not None)),
-        name='lamb_' + kind,
-        in_specs=[hbm] * 4 + [vm] * (len(ins) - 4),
-        out_specs=[hbm] * 3 + [vm],
-        out_shape=[f, f, f, o_shape],
+        functools.partial(lamb_kernel, kind, part, p, nb, size, len(g), int(h is not None), int(y is not None)),
+        name=f'lamb_{kind}_{part}',
+        in_specs=specs,
+        out_specs=[hbm] * 3 + [vm] * (1 + len(loss)),
+        out_shape=[f, f, f, o_shape] + loss,
         scratch_shapes=[pltpu.VMEM((nbuf, 3) + blk, F32), pltpu.VMEM((nbuf,) + gblk, BF), pltpu.VMEM((nbuf, 3) + blk, F32),
                         pltpu.SemaphoreType.DMA((nbuf, 4)), pltpu.SemaphoreType.DMA((nbuf, 3))],
+        input_output_aliases=alias,
         compiler_params=pltpu.CompilerParams(vmem_limit_bytes=52 * 2 ** 20),
-        cost_estimate=pl.CostEstimate(flops=40 * 10 ** 9, bytes_accessed=rows * cols * 26, transcendentals=0),
+        cost_estimate=pl.CostEstimate(flops=25 * 10 ** 8 * nb, bytes_accessed=nb * 26 * size * 1024, transcendentals=0),
     )(*ins)
 
 
@@ -558,14 +608,16 @@
 
     def step(wi, w1, w2, mi, vi, m1, v1, m2, v2, x0, y0, x1, y1):
         w1, w2, m1, v1, m2, v2 = (t[0] for t in (w1, w2, m1, v1, m2, v2))
-        d = wi.shape[1]
-        s2, s1, gi, c = reduce_grads(p, x0, y0, w2, m2, v2, w1, m1, v1, wi, mi, vi)
+        s2, s1, gi, n2, n1, c = reduce_grads(p, x0, y0, w2, m2, v2, w1, m1, v1, wi, mi, vi)
         g1 = gather(s1)
         g2 = gather(s2)
-        wi_n, mi_n, vi_n, h = lamb('in', wi, mi, vi, gi, c[1], x1)
-        w1_n, m1_n, v1_n, s = lamb('cols', w1, m1, v1, g1, c[2], h.astype(BF))
-        w2_n, m2_n, v2_n, h = lamb('out', w2, m2, v2, g2, c[0], s, h)
-        loss = jnp.sum((h - y1.astype(F32)) ** 2, axis=-1) / (2.0 * d)
+        wi_n, mi_n, vi_n, h = lamb('in', 'all', p, wi, mi, vi, [gi], c[1], x1, size=128, nbuf=8)
+        hb = h.astype(BF)
+        *u, s = lamb('cols', 'near', p, w1, m1, v1, [s1, n1], c[2], hb)
+        w1_n, m1_n, v1_n, s = lamb('cols', 'far', p, w1, m1, v1, [g1], c[2], hb, h=s, prev=u)
+        *u, h = lamb('out', 'near', p, w2, m2, v2, [s2, n2], c[0], s, h=h)
+        w2_n, m2_n, v2_n, h, loss = lamb('out', 'far', p, w2, m2, v2, [g2], c[0], s, h=h, y=y1, prev=u)
+        loss = loss[0]
         return (wi_n, w1_n[None], w2_n[None], mi_n, vi_n, m1_n[None], v1_n[None], m2_n[None], v2_n[None], loss, h)
 
     w2s = P('rep', None)

time: 423 us -> 415 us (0.981)
  waiting for transfers between devices: 17.6 us -> 0.83 us
  Pallas kernels: 388 us -> 398 us
    all_gather x2, waiting for transfers between devices: 16.9 us -> 0.04 us  [gather(): return lax.all_gather(s, 'data', axis=0, tiled=True)]
    pallas_call x3 -> x5, Pallas kernels: 118 us -> 127 us  [lamb(): pl.pallas_call(functools.partial(lamb_kernel, kind, part, p, nb, size, le...]
  transfers between devices with their start and end apart: 2 -> 2, of which waited for: 2 -> 0; matrix products, arithmetic and copies ran while one was open for 0% -> 0% of each run, Pallas kernels for 19% -> 23%
where the time goes in v3:
time: 415 us; the launch traced here: 414 us
  Pallas kernels  398 us (96%)
  between operations  14.2 us (3%)
    pallas_call x1, Pallas kernels, reduce_grads(): pl.pallas_call(functools.partial(sum_kernel, p), name='sum_grads', in_spe...  270 us
    pallas_call x5, Pallas kernels, lamb(): pl.pallas_call(functools.partial(lamb_kernel, kind, part, p, nb, size, le...  127 us
  transfers between devices with their start and end apart: 2, of which 0 were waited for; matrix products, arithmetic and copies ran while one was open for 0% of the time, Pallas kernels for 23%

profile of v3, /device:TPU:81, one launch (start us, length us, event | category | flops | bytes accessed | tf_op | source)
XLA Modules:
  0.0 414.0 jit_solution(17181324846552592015)
XLA Ops:
  7.2 0.1 all-gather.3.cloned.1.call-start
  7.3 270.1 %sum_grads.1 = (bf16[512,1024]{1,0:T(8,128)(2,1)}, bf16[512,1024]{1,0:T(8,128)(2,1)}, bf16[4096,1024]{1,0:T(8,128)(2,1)}, bf16[512,1024]{1,0:T(8,128)(2,1)}, bf1...) custom-call(bf16[256,4096]{1,0:T(8,128)(2,1)} %x_ref.1, bf16[256,1024]{1,0:T(8,128)(2,1)} %y_ref.1, f32[4096,1024]{1,0:T(8,128)} %bitcast.28, ...), custom_call_target="tpu_custom_call" | custom-call | flops 99999997952 | bytes 100000000 | tf_op jit(solution)/shard_map/sum_grads/pallas_call | solution.py:432
  277.4 0.1 all-gather.3.cloned.1.call-update
  277.5 0.1 all-gather.5.cloned.1.call-start
  277.5 0.7 all-gather.5.cloned.1.call-update
  278.3 0.7 slice_bitcast_fusion
  278.9 0.0 copy-start.1
  279.0 39.1 %lamb_in_all.1 = (f32[4096,1024]{1,0:T(8,128)}, f32[4096,1024]{1,0:T(8,128)}, f32[4096,1024]{1,0:T(8,128)}, f32[256,1024]{1,0:T(8,128)S(1)}) custom-call(f32[4096,1024]{1,0:T(8,128)} %w.1, f32[4096,1024]{1,0:T(8,128)} %m.1, f32[4096,1024]{1,0:T(8,128)} %v.1, bf16[4096,1024]{1,0:T(8,128)(2,1)} %get-tuple-element.38.refs_0_, ...), custom_call_target="tpu_custom_call" | custom-call | flops 80000000000 | bytes 109051904 | tf_op jit(solution)/shard_map/lamb_in_all/pallas_call | solution.py:589
  318.1 0.0 copy-start
  318.1 0.1 convert_element_type.3.refs_3_.refs_2_
  318.2 0.0 copy-done.1
  318.2 12.3 %lamb_cols_near.1 = (f32[1024,4096]{1,0:T(8,128)}, f32[1024,4096]{1,0:T(8,128)}, f32[1024,4096]{1,0:T(8,128)}, bf16[256,4096]{1,0:T(8,128)(2,1)}) custom-call(f32[1024,4096]{1,0:T(8,128)} %bitcast.20, f32[1024,4096]{1,0:T(8,128)} %bitcast.23, f32[1024,4096]{1,0:T(8,128)} %bitcast.26, bf16[512,1024]{1,0:T(8,128)(2,1)S(1)} %copy-done.1, ...), custom_call_target="tpu_custom_call" | custom-call | flops 10000000000 | bytes 27262976 | tf_op jit(solution)/shard_map/lamb_cols_near/pallas_call | solution.py:589
  330.5 0.0 copy-done
  330.5 0.0 all-gather.3.cloned.1.call-done.refs_0_
  330.6 32.4 %lamb_cols_far.1 = (f32[1024,4096]{1,0:T(8,128)}, f32[1024,4096]{1,0:T(8,128)}, f32[1024,4096]{1,0:T(8,128)}, bf16[256,4096]{1,0:T(8,128)(2,1)}) custom-call(f32[1024,4096]{1,0:T(8,128)} %bitcast.21, f32[1024,4096]{1,0:T(8,128)} %bitcast.24, f32[1024,4096]{1,0:T(8,128)} %bitcast.27, ...), custom_call_target="tpu_custom_call", output_to_operand_aliasing={{0}: (7, {}), {1}: (8, {}), {2}: (9, {})} | custom-call | flops 30000001024 | bytes 81788928 | tf_op jit(solution)/shard_map/lamb_cols_far/pallas_call | solution.py:589
  363.0 0.0 copy-start.2
  363.0 13.1 %lamb_out_near.1 = (f32[4096,1024]{1,0:T(8,128)}, f32[4096,1024]{1,0:T(8,128)}, f32[4096,1024]{1,0:T(8,128)}, f32[256,1024]{1,0:T(8,128)S(1)}) custom-call(f32[4096,1024]{1,0:T(8,128)} %bitcast.29, f32[4096,1024]{1,0:T(8,128)} %bitcast.32, f32[4096,1024]{1,0:T(8,128)} %bitcast.35, bf16[512,1024]{1,0:T(8,128)(2,1)} %get-tuple-element.49.refs_0_, ...), custom_call_target="tpu_custom_call" | custom-call | flops 10000000000 | bytes 27262976 | tf_op jit(solution)/shard_map/lamb_out_near/pallas_call | solution.py:589
  376.1 0.0 all-gather.5.cloned.1.call-done.refs_0_
  376.2 0.0 copy-done.2
  376.2 30.4 %lamb_out_far.1 = (f32[4096,1024]{1,0:T(8,128)}, f32[4096,1024]{1,0:T(8,128)}, f32[4096,1024]{1,0:T(8,128)}, f32[256,1024]{1,0:T(8,128)}, f32[8,256]{1,0:T(8,128)S(1)}) custom-call(f32[4096,1024]{1,0:T(8,128)} %bitcast.30, f32[4096,1024]{1,0:T(8,128)} %bitcast.33, ...), custom_call_target="tpu_custom_call", output_to_operand_aliasing={{0}: (8, {}), {1}: (9, {}), {2}: (10, {})} | custom-call | flops 30000001024 | bytes 81788928 | tf_op jit(solution)/shard_map/lamb_out_far/pallas_call | solution.py:589
  406.6 0.6 slice.17
Async XLA Ops:
  7.2 323.4 %all-gather.3.cloned.1.call-start = ((), (), s32[]{:S(2)}) async-start(), calls=%async_computation | async-start | bytes 9437184 | tf_op jit(solution)/shard_map/all_gather | solution.py:607
  277.5 98.7 %all-gather.5.cloned.1.call-start = ((), (), s32[]{:S(2)}) async-start(), calls=%async_computation.1 | async-start | bytes 9437184 | tf_op jit(solution)/shard_map/all_gather | solution.py:607
  278.9 39.2 %copy-start.1 = (bf16[512,1024]{1,0:T(8,128)(2,1)S(1)}, bf16[512,1024]{1,0:T(8,128)(2,1)}, u32[]{:S(2)}) copy-start(bf16[512,1024]{1,0:T(8,128)(2,1)} %get-tuple-element.41.refs_0_) | copy-start | bytes 3145732
  318.1 12.4 %copy-start = (f32[256,1024]{1,0:T(8,128)}, f32[256,1024]{1,0:T(8,128)S(1)}, u32[]{:S(2)}) copy-start(f32[256,1024]{1,0:T(8,128)S(1)} %get-tuple-element.42.refs_4_) | copy-start | bytes 3145732
  363.0 13.2 %copy-start.2 = (bf16[256,1024]{1,0:T(8,128)(2,1)S(1)}, bf16[256,1024]{1,0:T(8,128)(2,1)}, u32[]{:S(2)}) copy-start(bf16[256,1024]{1,0:T(8,128)(2,1)} %refs_4_.1) | copy-start | bytes 1572868
Sparse Core Ops, SparseCore 0:
  277.6 48.8 all-gather.2
  328.1 46.7 all-gather.4

commit v4 on v3

--- a/solution.py
+++ b/solution.py
@@ -450,29 +450,26 @@
     )(x, y, w2, m2, v2, w1, m1, v1, wi, mi, vi)
 
 
-def lamb_kernel(kind, part, p, nb, size, n_g, has_h, has_y, w, m, v, *refs):
-    g_refs, refs = refs[:n_g], refs[n_g:]
-    c_ref, x_ref, refs = refs[0], refs[1], refs[2:]
-    h_ref = refs[0] if has_h else None
-    y_ref = refs[has_h] if has_y else None
-    l_ref, refs = (refs[-6], refs[:-6] + refs[-5:]) if has_y else (None, refs)
-    wo, mo, vo, o_ref, ib, gb, ob, i_sem, o_sem = refs[-9:]
+def lamb_stage(kind, part, p, nb, w, m, v, g_refs, c_ref, outs, bufs, get_x, put):
+    ib, gb, ob, i_sem, o_sem = bufs
     nbuf = ib.shape[0]
-    grows = gb.shape[1]
     me = lax.axis_index('data')
     core = lax.rem(me, 2)
+    c = c_ref[0:1, 0:1]
 
     def which(i):
         if part == 'all':
             return i
-        h = lax.rem(i, 2)
         if part == 'near':
-            return 2 * (me + lax.div(i, 2) * (1 - 2 * core)) + h
+            return 2 * (me + lax.div(i, 2) * (1 - 2 * core)) + lax.rem(i, 2)
         chip = lax.rem(lax.div(me, 2) + 1 + lax.div(i, 4), p // 2)
         return 4 * chip + lax.rem(i, 4)
 
+    def span(i):
+        return pl.ds(pl.multiple_of(i * 256, 256), 256)
+
     def at(i):
-        s = pl.ds(pl.multiple_of(which(i) * size, size), size)
+        s = span(which(i))
         return (slice(None), s) if kind == 'cols' else (s, slice(None))
 
     def loads(i):
@@ -481,8 +478,7 @@
 
     def load_g(i, ref, j):
         b = lax.rem(i, nbuf)
-        rows = pl.ds(pl.multiple_of(j * grows, grows), grows)
-        return pltpu.make_async_copy(ref.at[rows], gb.at[b], i_sem.at[b, 3])
+        return pltpu.make_async_copy(ref.at[span(j)], gb.at[b], i_sem.at[b, 3])
 
     def start(i):
         for t in loads(i):
@@ -497,106 +493,144 @@
 
     def stores(i):
         b = lax.rem(i, nbuf)
-        return [pltpu.make_async_copy(ob.at[b, n], r.at[at(i)], o_sem.at[b, n]) for n, r in enumerate((wo, mo, vo))]
-
+        return [pltpu.make_async_copy(ob.at[b, n], r.at[at(i)], o_sem.at[b, n]) for n, r in enumerate(outs)]
+
+    def run(start_next=None):
+        def block(i, _):
+            b = lax.rem(i, nbuf)
+            for t in loads(i):
+                t.wait()
+            load_g(i, g_refs[0], 0).wait()
+
+            @pl.when(i >= nbuf)
+            def _():
+                for t in stores(i - nbuf):
+                    t.wait()
+
+            def update(grow, gcol, rows, cols):
+                w_t = ib[b, 0, rows, cols]
+                m2, v2, u = moments(w_t, gb[b, grow, gcol].astype(F32), ib[b, 1, rows, cols], ib[b, 2, rows, cols])
+                ob[b, 0, rows, cols] = w_t - c * u
+                ob[b, 1, rows, cols] = m2
+                ob[b, 2, rows, cols] = v2
+
+            def piece(n, _):
+                for q in range(4):
+                    lanes = pl.ds(q * 256, 256)
+                    off = pl.multiple_of(n * 64, 64)
+                    if kind == 'cols':
+                        update(pl.ds(off, 64), lanes, pl.ds(q * 256 + off, 64), slice(None))
+                    else:
+                        update(pl.ds(off, 64), lanes, pl.ds(off, 64), lanes)
+                return 0
+
+            lax.fori_loop(0, 4, piece, 0)
+            for t in stores(i):
+                t.start()
+
+            @pl.when(i + nbuf < nb)
+            def _():
+                start(i + nbuf)
+
+            if start_next is not None:
+                @pl.when(i + nbuf >= nb)
+                def _():
+                    start_next(i + nbuf - nb)
+
+            s = span(which(i))
+            put(i, s, jnp.dot(get_x(s), ob[b, 0].astype(BF), preferred_element_type=F32))
+            return 0
+
+        lax.fori_loop(0, nb, block, 0)
+
+    def drain():
+        for i in range(nb - nbuf, nb):
+            for t in stores(i):
+                t.wait()
+
+    return start, run, drain
+
+
+def adder(o_ref, h_ref=None):
+    def put(i, s, d):
+        @pl.when(i == 0)
+        def _():
+            o_ref[...] = d if h_ref is None else h_ref[...] + d
+
+        @pl.when(i > 0)
+        def _():
+            o_ref[...] += d
+    return put
+
+
+def setter(o_ref):
+    def put(i, s, d):
+        o_ref[:, s] = gelu(d).astype(BF)
+    return put
+
+
+def lamb_a(p, wi, mi, vi, gi, w1, m1, v1, s1, n1, ci, c1, x_ref, wio, mio, vio, w1o, m1o, v1o, h_ref, s_ref, hb, *bufs):
+    nbuf = bufs[0].shape[0]
+    start, run, drain = lamb_stage('in', 'all', p, wi.shape[0] // 256, wi, mi, vi, (gi,), ci, (wio, mio, vio), bufs[:5],
+                                   lambda s: x_ref[:, s], adder(h_ref))
+    start2, run2, drain2 = lamb_stage('cols', 'near', p, 4, w1, m1, v1, (s1, n1), c1, (w1o, m1o, v1o), bufs[5:],
+                                      lambda s: hb[...], setter(s_ref))
     for i in range(nbuf):
         start(jnp.int32(i))
-    c = c_ref[0:1, 0:1]
-    if kind == 'cols' and has_h:
-        o_ref[...] = h_ref[...]
-
-    def block(i, _):
-        b = lax.rem(i, nbuf)
-        for t in loads(i):
-            t.wait()
-        load_g(i, g_refs[0], 0).wait()
-
-        @pl.when(i >= nbuf)
-        def _():
-            for t in stores(i - nbuf):
-                t.wait()
-
-        def update(grow, gcol, rows, cols):
-            w_t = ib[b, 0, rows, cols]
-            m2, v2, u = moments(w_t, gb[b, grow, gcol].astype(F32), ib[b, 1, rows, cols], ib[b, 2, rows, cols])
-            ob[b, 0, rows, cols] = w_t - c * u
-            ob[b, 1, rows, cols] = m2
-            ob[b, 2, rows, cols] = v2
-
-        def piece(n, _):
-            for q in range(4):
-                lanes = pl.ds(q * 256, 256)
-                off = pl.multiple_of(n * 64, 64)
-                if kind == 'cols':
-                    update(pl.ds(off, 64), lanes, pl.ds(q * 256 + off, 64), slice(None))
-                else:
-                    update(pl.ds(off, 64), lanes, pl.ds(off, 64), lanes)
-            return 0
-
-        lax.fori_loop(0, grows // 64, piece, 0)
-        for t in stores(i):
-            t.start()
-
-        @pl.when(i + nbuf < nb)
-        def _():
-            start(i + nbuf)
-
-        x = x_ref[...] if kind == 'cols' else x_ref[:, at(i)[0]]
-        d = jnp.dot(x, ob[b, 0].astype(BF), preferred_element_type=F32)
-        if kind == 'cols':
-            o_ref[:, at(i)[1]] = gelu(d).astype(BF)
-        else:
-            @pl.when(i == 0)
-            def _():
-                o_ref[...] = h_ref[...] + d if has_h else d
-
-            @pl.when(i > 0)
-            def _():
-                o_ref[...] += d
-        return 0
-
-    lax.fori_loop(0, nb, block, 0)
-    if has_y:
-        e = o_ref[...] - y_ref[...].astype(F32)
-        row = jnp.sum(e * e, axis=-1, keepdims=True) / (2.0 * e.shape[1])
-        l_ref[...] = jnp.broadcast_to(row, (e.shape[0], 128)).T[0:8]
-    for i in range(nb - nbuf, nb):
-        for t in stores(i):
-            t.wait()
-
-
-def lamb(kind, part, p, w, m, v, g, c, x, h=None, y=None, prev=None, size=256, nbuf=4):
-    rows, cols = w.shape
-    tok = x.shape[0]
+    run(start2)
+    hb[...] = h_ref[...].astype(BF)
+    run2()
+    drain()
+    drain2()
+
+
+def lamb_b(p, w1, m1, v1, g1, w2, m2, v2, s2, n2, pw, pm, pv, c1, c2, h0_ref, s0_ref,
+           w1o, m1o, v1o, w2o, m2o, v2o, s_ref, h_ref, hb, *bufs):
+    nbuf = bufs[0].shape[0]
+    start, run, drain = lamb_stage('cols', 'far', p, w1.shape[1] // 256 - 4, w1, m1, v1, (g1,), c1, (w1o, m1o, v1o), bufs[:5],
+                                   lambda s: hb[...], setter(s_ref))
+    start2, run2, drain2 = lamb_stage('out', 'near', p, 4, w2, m2, v2, (s2, n2), c2, (w2o, m2o, v2o), bufs[5:],
+                                      lambda s: s_ref[:, s], adder(h_ref, h0_ref))
+    for i in range(nbuf):
+        start(jnp.int32(i))
+    s_ref[...] = s0_ref[...]
+    hb[...] = h0_ref[...].astype(BF)
+    run(start2)
+    run2()
+    drain()
+    drain2()
+
+
+def lamb_c(p, w2, m2, v2, g2, pw, pm, pv, c2, s_ref, h0_ref, y_ref, w2o, m2o, v2o, h_ref, l_ref, *bufs):
+    start, run, drain = lamb_stage('out', 'far', p, w2.shape[0] // 256 - 4, w2, m2, v2, (g2,), c2, (w2o, m2o, v2o), bufs,
+                                   lambda s: s_ref[:, s], adder(h_ref, h0_ref))
+    for i in range(bufs[0].shape[0]):
+        start(jnp.int32(i))
+    run()
+    e = h_ref[...] - y_ref[...].astype(F32)
+    row = jnp.sum(e * e, axis=-1, keepdims=True) / (2.0 * e.shape[1])
+    l_ref[...] = jnp.broadcast_to(row, (e.shape[0], 128)).T[0:8]
+    drain()
+
+
+def lamb_call(body, name, p, n_hbm, out_hbm, out_vm, kinds, nbuf, blocks, alias, *ins):
     hbm = pl.BlockSpec(memory_space=pltpu.HBM)
     vm = pl.BlockSpec(memory_space=pltpu.VMEM)
-    if kind == 'cols':
-        nb, blk, gblk = cols // size, (rows, size), (256, 1024)
-        o_shape = jax.ShapeDtypeStruct((tok, cols), BF)
-    else:
-        nb, blk, gblk = rows // size, (size, cols), (size, cols)
-        o_shape = jax.ShapeDtypeStruct((tok, cols), F32)
-    nb = {'all': nb, 'near': nb // (p // 2), 'far': nb - nb // (p // 2)}[part]
-    ins = [w, m, v, *g, c, x] + [t for t in (h, y) if t is not None]
-    specs = [hbm] * (3 + len(g)) + [vm] * (len(ins) - 3 - len(g))
-    alias = {}
-    for k, t in enumerate(prev or ()):
-        alias[len(ins)] = k
-        ins.append(t)
-        specs.append(hbm)
-    f = jax.ShapeDtypeStruct((rows, cols), F32)
-    loss = [] if y is None else [jax.ShapeDtypeStruct((8, tok), F32)]
+    tok = ins[-1].shape[0]
+    scratch = [pltpu.VMEM((tok, 1024), BF)] if len(kinds) > 1 else []
+    for k in kinds:
+        blk = (1024, 256) if k == 'cols' else (256, 1024)
+        scratch += [pltpu.VMEM((nbuf, 3) + blk, F32), pltpu.VMEM((nbuf, 256, 1024), BF), pltpu.VMEM((nbuf, 3) + blk, F32),
+                    pltpu.SemaphoreType.DMA((nbuf, 4)), pltpu.SemaphoreType.DMA((nbuf, 3))]
     return pl.pallas_call(
-        functools.partial(lamb_kernel, kind, part, p, nb, size, len(g), int(h is not None), int(y is not None)),
-        name=f'lamb_{kind}_{part}',
-        in_specs=specs,
-        out_specs=[hbm] * 3 + [vm] * (1 + len(loss)),
-        out_shape=[f, f, f, o_shape] + loss,
-        scratch_shapes=[pltpu.VMEM((nbuf, 3) + blk, F32), pltpu.VMEM((nbuf,) + gblk, BF), pltpu.VMEM((nbuf, 3) + blk, F32),
-                        pltpu.SemaphoreType.DMA((nbuf, 4)), pltpu.SemaphoreType.DMA((nbuf, 3))],
+        functools.partial(body, p), name=name,
+        in_specs=[hbm] * n_hbm + [vm] * (len(ins) - n_hbm),
+        out_specs=[hbm] * len(out_hbm) + [vm] * len(out_vm),
+        out_shape=[jax.ShapeDtypeStruct(t.shape, F32) for t in out_hbm] + list(out_vm),
+        scratch_shapes=scratch,
         input_output_aliases=alias,
-        compiler_params=pltpu.CompilerParams(vmem_limit_bytes=52 * 2 ** 20),
-        cost_estimate=pl.CostEstimate(flops=25 * 10 ** 8 * nb, bytes_accessed=nb * 26 * size * 1024, transcendentals=0),
+        compiler_params=pltpu.CompilerParams(vmem_limit_bytes=54 * 2 ** 20),
+        cost_estimate=pl.CostEstimate(flops=25 * 10 ** 8 * blocks, bytes_accessed=blocks * 26 * 2 ** 18, transcendentals=0),
     )(*ins)
 
 
@@ -611,12 +645,19 @@
         s2, s1, gi, n2, n1, c = reduce_grads(p, x0, y0, w2, m2, v2, w1, m1, v1, wi, mi, vi)
         g1 = gather(s1)
         g2 = gather(s2)
-        wi_n, mi_n, vi_n, h = lamb('in', 'all', p, wi, mi, vi, [gi], c[1], x1, size=128, nbuf=8)
-        hb = h.astype(BF)
-        *u, s = lamb('cols', 'near', p, w1, m1, v1, [s1, n1], c[2], hb)
-        w1_n, m1_n, v1_n, s = lamb('cols', 'far', p, w1, m1, v1, [g1], c[2], hb, h=s, prev=u)
-        *u, h = lamb('out', 'near', p, w2, m2, v2, [s2, n2], c[0], s, h=h)
-        w2_n, m2_n, v2_n, h, loss = lamb('out', 'far', p, w2, m2, v2, [g2], c[0], s, h=h, y=y1, prev=u)
+        tok, d = y0.shape
+        hs = jax.ShapeDtypeStruct((tok, d), F32)
+        ss = jax.ShapeDtypeStruct((tok, w1.shape[1]), BF)
+        ls = jax.ShapeDtypeStruct((8, tok), F32)
+        wi_n, mi_n, vi_n, *u, h, s = lamb_call(
+            lamb_a, 'lamb_a', p, 9, (wi, mi, vi, w1, m1, v1), (hs, ss), ('in', 'cols'), 3, 20, {},
+            wi, mi, vi, gi, w1, m1, v1, s1, n1, c[1], c[2], x1)
+        w1_n, m1_n, v1_n, *u, s, h = lamb_call(
+            lamb_b, 'lamb_b', p, 12, (w1, m1, v1, w2, m2, v2), (ss, hs), ('cols', 'out'), 3, 16, {9: 0, 10: 1, 11: 2},
+            w1, m1, v1, g1, w2, m2, v2, s2, n2, *u, c[2], c[0], h, s)
+        w2_n, m2_n, v2_n, h, loss = lamb_call(
+            lamb_c, 'lamb_c', p, 7, (w2, m2, v2), (hs, ls), ('out',), 4, 12, {4: 0, 5: 1, 6: 2},
+            w2, m2, v2, g2, *u, c[0], s, h, y1)
         loss = loss[0]
         return (wi_n, w1_n[None], w2_n[None], mi_n, vi_n, m1_n[None], v1_n[None], m2_n[None], v2_n[None], loss, h)
 

time: 415 us -> 414 us (level)
  Pallas kernels: 398 us -> 392 us
    pallas_call x5 -> x3, Pallas kernels: 127 us -> 122 us  [lamb_call(): pl.pallas_call(functools.partial(body, p), name=name, in_specs=[hbm] * n_...]
  transfers between devices with their start and end apart: 2 -> 2, of which waited for: 0 -> 1; matrix products, arithmetic and copies ran while one was open for 0% -> 0% of each run, Pallas kernels for 23% -> 22%
where the time goes in v4:
time: 414 us
  Pallas kernels  392 us (95%)
  between operations  14.1 us (3%)
  waiting for transfers between devices  4.51 us (1%)
    pallas_call x1, Pallas kernels, reduce_grads(): pl.pallas_call(functools.partial(sum_kernel, p), name='sum_grads', in_spe...  270 us
    pallas_call x3, Pallas kernels, lamb_call(): pl.pallas_call(functools.partial(body, p), name=name, in_specs=[hbm] * n_...  122 us
  transfers between devices with their start and end apart: 2, of which 1 were waited for; matrix products, arithmetic and copies ran while one was open for 0% of the time, Pallas kernels for 22%

profile of v4, /device:TPU:81, one launch (start us, length us, event | category | flops | bytes accessed | tf_op | source)
XLA Modules:
  0.0 413.8 jit_solution(8040365649073209330)
XLA Ops:
  7.2 0.1 all-gather.3.cloned.1.call-start
  7.3 270.1 %sum_grads.1 = (bf16[512,1024]{1,0:T(8,128)(2,1)}, bf16[512,1024]{1,0:T(8,128)(2,1)}, bf16[4096,1024]{1,0:T(8,128)(2,1)}, bf16[512,1024]{1,0:T(8,128)(2,1)}, bf1...) custom-call(bf16[256,4096]{1,0:T(8,128)(2,1)} %x_ref.2, bf16[256,1024]{1,0:T(8,128)(2,1)} %y_ref.2, f32[4096,1024]{1,0:T(8,128)} %bitcast.19, ...), custom_call_target="tpu_custom_call" | custom-call | flops 99999997952 | bytes 100000000 | tf_op jit(solution)/shard_map/sum_grads/pallas_call | solution.py:432
  277.4 0.1 all-gather.3.cloned.1.call-update
  277.4 0.1 all-gather.5.cloned.1.call-start
  277.5 0.7 all-gather.5.cloned.1.call-update
  278.3 1.3 slice_bitcast_fusion
  279.5 49.3 %lamb_a.1 = (f32[4096,1024]{1,0:T(8,128)}, f32[4096,1024]{1,0:T(8,128)}, f32[4096,1024]{1,0:T(8,128)}, f32[1024,4096]{1,0:T(8,128)}, f32[1024,4096]{1,0:T(8,128)...) custom-call(f32[4096,1024]{1,0:T(8,128)} %wi.3, f32[4096,1024]{1,0:T(8,128)} %mi.3, ...), custom_call_target="tpu_custom_call" | custom-call | flops 49999998976 | bytes 136314880 | tf_op jit(solution)/shard_map/lamb_a/pallas_call | solution.py:625
  328.9 0.0 all-gather.3.cloned.1.call-done.g1
  328.9 42.2 %lamb_b.1 = (f32[1024,4096]{1,0:T(8,128)}, f32[1024,4096]{1,0:T(8,128)}, f32[1024,4096]{1,0:T(8,128)}, f32[4096,1024]{1,0:T(8,128)}, f32[4096,1024]{1,0:T(8,128)...) custom-call(f32[1024,4096]{1,0:T(8,128)} %bitcast.30, ...), custom_call_target="tpu_custom_call", output_to_operand_aliasing={{0}: (9, {}), {1}: (10, {}), {2}: (11, {})} | custom-call | flops 40000000000 | bytes 109051904 | tf_op jit(solution)/shard_map/lamb_b/pallas_call | solution.py:625
  371.1 3.7 all-gather.5.cloned.1.call-done.g2
  374.8 30.8 %lamb_c.1 = (f32[4096,1024]{1,0:T(8,128)}, f32[4096,1024]{1,0:T(8,128)}, f32[4096,1024]{1,0:T(8,128)}, f32[256,1024]{1,0:T(8,128)}, f32[8,256]{1,0:T(8,128)}) custom-call(f32[4096,1024]{1,0:T(8,128)} %bitcast.21, f32[4096,1024]{1,0:T(8,128)} %bitcast.24, f32[4096,1024]{1,0:T(8,128)} %bitcast.27, ...), custom_call_target="tpu_custom_call", output_to_operand_aliasing={{0}: (4, {}), {1}: (5, {}), {2}: (6, {})} | custom-call | flops 30000001024 | bytes 81788928 | tf_op jit(solution)/shard_map/lamb_c/pallas_call | solution.py:625
  405.7 1.3 slice.17
Async XLA Ops:
  7.2 321.7 %all-gather.3.cloned.1.call-start = ((), (), s32[]{:S(2)}) async-start(), calls=%async_computation | async-start | bytes 9437184 | tf_op jit(solution)/shard_map/all_gather | solution.py:641
  277.4 97.4 %all-gather.5.cloned.1.call-start = ((), (), s32[]{:S(2)}) async-start(), calls=%async_computation.1 | async-start | bytes 9437184 | tf_op jit(solution)/shard_map/all_gather | solution.py:641
Sparse Core Ops, SparseCore 0:
  277.6 48.8 all-gather.2
  328.1 46.7 all-gather.4

commit v5 on v4

--- a/solution.py
+++ b/solution.py
@@ -44,9 +44,9 @@
 
 
 def sum_kernel(p, x_ref, y_ref, w2, m2, v2, w1, m1, v1, wi, mi, vi,
-               o2, o1, oi, p2, p1, cs_ref,
+               o2, o1, oi, p2, p1, qa, qb, cs_ref,
                s_ref, gb_ref, hb_ref, a_ref, g_ref, st, pr, pt, rb, e_s, h_t, g0_s, wa, wb, lw, gst, ns, nr,
-               d_send, d_recv, r_send, r_recv, credit, pcredit, w_sem, l_sem, o_sem, n_send, n_recv, a_send, a_recv, b_send, b_recv, f_sem, c_send, c_recv):
+               d_send, d_recv, r_send, r_recv, credit, pcredit, w_sem, l_sem, o_sem, n_send, n_recv, a_send, a_recv, b_send, b_recv, f_sem, c_send, c_recv, q_sem):
     me = lax.axis_index('data')
     core = lax.rem(me, 2)
     chip = lax.div(me, 2)
@@ -157,6 +157,9 @@
         rows = pl.ds(h * 256, 256)
         dst = oi.at[block(me, h)] if k == 1 else (o2, oi, o1)[k].at[rows]
         return pltpu.make_async_copy(gst.at[k, rows], dst, o_sem.at[k, h])
+
+    def half_out(h):
+        return pltpu.make_async_copy(gst.at[0, pl.ds(h * 256, 256)], (qa, qb)[h], q_sem.at[h])
 
     def give(k, h):
         rows = pl.ds(h * 256, 256)
@@ -397,6 +400,8 @@
             ag_own(r % 2)
         else:
             give(r // 2, r % 2).start()
+        if r < 2:
+            half_out(r).start()
 
     def norm(o):
         return remote(ns, nr.at[me], n_send.at[o - 1], n_recv.at[o - 1], lax.rem(me + o, p))
@@ -421,6 +426,8 @@
         ag_pair(n).wait()
     for n in range(4):
         give(n // 2 * 2, n % 2).wait()
+    for h in range(2):
+        half_out(h).wait()
 
 
 def reduce_grads(p, x, y, w2, m2, v2, w1, m1, v1, wi, mi, vi):
@@ -433,8 +440,8 @@
         functools.partial(sum_kernel, p),
         name='sum_grads',
         in_specs=[vm] * 2 + [hbm] * 9,
-        out_specs=[hbm] * 5 + [vm],
-        out_shape=[o, o, jax.ShapeDtypeStruct((512 * p, 1024), BF), o, o, jax.ShapeDtypeStruct((3, 8, 128), F32)],
+        out_specs=[hbm] * 7 + [vm],
+        out_shape=[o, o, jax.ShapeDtypeStruct((512 * p, 1024), BF), o, o] + [jax.ShapeDtypeStruct((256, 1024), BF)] * 2 + [jax.ShapeDtypeStruct((3, 8, 128), F32)],
         scratch_shapes=[
             pltpu.VMEM((tok, 4096), BF), pltpu.VMEM((tok, 1024), BF), pltpu.VMEM((tok, 1024), BF),
             pltpu.VMEM((tok, 4096), F32), pltpu.VMEM((tok, 1024), F32),
@@ -443,7 +450,7 @@
             pltpu.VMEM((tok, 1024), BF), pltpu.VMEM((2, 256, 1024), F32), pltpu.VMEM((2, 128, 4096), F32),
             pltpu.VMEM((3, 256, 1024), F32), pltpu.VMEM((3, 512, 1024), BF), pltpu.VMEM((48, 128), F32), pltpu.VMEM((p, 48, 128), F32),
             dma((2, 4)), dma((2, 4)), dma((2, 6)), dma((2, 6)), reg((2,)), reg, dma((2,)), dma((3, 4)), dma((3, 2)),
-            dma((p - 1,)), dma((p - 1,)), dma((6,)), dma((6,)), dma((8,)), dma((8,)), dma((4, 2)), dma((2, 2)), dma((2, 2)),
+            dma((p - 1,)), dma((p - 1,)), dma((6,)), dma((6,)), dma((8,)), dma((8,)), dma((4, 2)), dma((2, 2)), dma((2, 2)), dma((2,)),
         ],
         compiler_params=pltpu.CompilerParams(collective_id=0, has_side_effects=True, vmem_limit_bytes=60 * 2 ** 20),
         cost_estimate=pl.CostEstimate(flops=10 ** 11, bytes_accessed=10 ** 8, transcendentals=0),
@@ -462,8 +469,13 @@
             return i
         if part == 'near':
             return 2 * (me + lax.div(i, 2) * (1 - 2 * core)) + lax.rem(i, 2)
-        chip = lax.rem(lax.div(me, 2) + 1 + lax.div(i, 4), p // 2)
-        return 4 * chip + lax.rem(i, 4)
+        if part == 'far':
+            chip = lax.rem(lax.div(me, 2) + 1 + lax.div(i, 4), p // 2)
+            return 4 * chip + lax.rem(i, 4)
+        return 2 * shard(i) + (part == 'far1')
+
+    def shard(i):
+        return 2 * lax.rem(lax.div(me, 2) + 1 + lax.div(i, 2), p // 2) + lax.rem(i, 2)
 
     def span(i):
         return pl.ds(pl.multiple_of(i * 256, 256), 256)
@@ -484,7 +496,7 @@
         for t in loads(i):
             t.start()
         if part != 'near':
-            load_g(i, g_refs[0], which(i)).start()
+            load_g(i, g_refs[0], shard(i) if part in ('far0', 'far1') else which(i)).start()
         else:
             for n in range(2):
                 @pl.when(lax.div(i, 2) == n)
@@ -601,15 +613,18 @@
     drain2()
 
 
-def lamb_c(p, w2, m2, v2, g2, pw, pm, pv, c2, s_ref, h0_ref, y_ref, w2o, m2o, v2o, h_ref, l_ref, *bufs):
-    start, run, drain = lamb_stage('out', 'far', p, w2.shape[0] // 256 - 4, w2, m2, v2, (g2,), c2, (w2o, m2o, v2o), bufs,
-                                   lambda s: s_ref[:, s], adder(h_ref, h0_ref))
-    for i in range(bufs[0].shape[0]):
+def lamb_c(half, p, w2, m2, v2, g2, pw, pm, pv, c2, s_ref, h0_ref, *refs):
+    y_ref, refs = (refs[0], refs[1:]) if half == 1 else (None, refs)
+    w2o, m2o, v2o, h_ref = refs[:4]
+    start, run, drain = lamb_stage('out', f'far{half}', p, w2.shape[0] // 512 - 2, w2, m2, v2, (g2,), c2, (w2o, m2o, v2o),
+                                   refs[-5:], lambda s: s_ref[:, s], adder(h_ref, h0_ref))
+    for i in range(refs[-5].shape[0]):
         start(jnp.int32(i))
     run()
-    e = h_ref[...] - y_ref[...].astype(F32)
-    row = jnp.sum(e * e, axis=-1, keepdims=True) / (2.0 * e.shape[1])
-    l_ref[...] = jnp.broadcast_to(row, (e.shape[0], 128)).T[0:8]
+    if half == 1:
+        e = h_ref[...] - y_ref[...].astype(F32)
+        row = jnp.sum(e * e, axis=-1, keepdims=True) / (2.0 * e.shape[1])
+        refs[4][...] = jnp.broadcast_to(row, (e.shape[0], 128)).T[0:8]
     drain()
 
 
@@ -642,9 +657,10 @@
 
     def step(wi, w1, w2, mi, vi, m1, v1, m2, v2, x0, y0, x1, y1):
         w1, w2, m1, v1, m2, v2 = (t[0] for t in (w1, w2, m1, v1, m2, v2))
-        s2, s1, gi, n2, n1, c = reduce_grads(p, x0, y0, w2, m2, v2, w1, m1, v1, wi, mi, vi)
+        s2, s1, gi, n2, n1, qa, qb, c = reduce_grads(p, x0, y0, w2, m2, v2, w1, m1, v1, wi, mi, vi)
         g1 = gather(s1)
-        g2 = gather(s2)
+        ga = gather(qa)
+        gb = gather(qb)
         tok, d = y0.shape
         hs = jax.ShapeDtypeStruct((tok, d), F32)
         ss = jax.ShapeDtypeStruct((tok, w1.shape[1]), BF)
@@ -655,9 +671,12 @@
         w1_n, m1_n, v1_n, *u, s, h = lamb_call(
             lamb_b, 'lamb_b', p, 12, (w1, m1, v1, w2, m2, v2), (ss, hs), ('cols', 'out'), 3, 16, {9: 0, 10: 1, 11: 2},
             w1, m1, v1, g1, w2, m2, v2, s2, n2, *u, c[2], c[0], h, s)
+        *u, h = lamb_call(
+            functools.partial(lamb_c, 0), 'lamb_c', p, 7, (w2, m2, v2), (hs,), ('out',), 4, 6, {4: 0, 5: 1, 6: 2},
+            w2, m2, v2, ga, *u, c[0], s, h)
         w2_n, m2_n, v2_n, h, loss = lamb_call(
-            lamb_c, 'lamb_c', p, 7, (w2, m2, v2), (hs, ls), ('out',), 4, 12, {4: 0, 5: 1, 6: 2},
-            w2, m2, v2, g2, *u, c[0], s, h, y1)
+            functools.partial(lamb_c, 1), 'lamb_d', p, 7, (w2, m2, v2), (hs, ls), ('out',), 4, 6, {4: 0, 5: 1, 6: 2},
+            w2, m2, v2, gb, *u, c[0], s, h, y1)
         loss = loss[0]
         return (wi_n, w1_n[None], w2_n[None], mi_n, vi_n, m1_n[None], v1_n[None], m2_n[None], v2_n[None], loss, h)
 

time: 414 us -> 417 us (level)
  Pallas kernels: 392 us -> 398 us
    pallas_call x3 -> x4, Pallas kernels: 122 us -> 128 us  [lamb_call(): pl.pallas_call(functools.partial(body, p), name=name, in_specs=[hbm] * n_...]
  transfers between devices with their start and end apart: 2 -> 3, of which waited for: 1 -> 0; matrix products, arithmetic and copies ran while one was open for 0% -> 0% of each run, Pallas kernels for 22% -> 26%
where the time goes in v5:
time: 417 us; the launch traced here: 416 us
  Pallas kernels  398 us (95%)
  between operations  13.8 us (3%)
    pallas_call x1, Pallas kernels, reduce_grads(): pl.pallas_call(functools.partial(sum_kernel, p), name='sum_grads', in_spe...  270 us
    pallas_call x4, Pallas kernels, lamb_call(): pl.pallas_call(functools.partial(body, p), name=name, in_specs=[hbm] * n_...  128 us
  transfers between devices with their start and end apart: 3, of which 0 were waited for; matrix products, arithmetic and copies ran while one was open for 0% of the time, Pallas kernels for 26%

profile of v5, /device:TPU:81, one launch (start us, length us, event | category | flops | bytes accessed | tf_op | source)
XLA Modules:
  0.0 416.1 jit_solution(16375275515262921554)
XLA Ops:
  7.2 0.1 all-gather.4.cloned.1.call-start
  7.3 270.1 %sum_grads.1 = (bf16[512,1024]{1,0:T(8,128)(2,1)}, bf16[512,1024]{1,0:T(8,128)(2,1)}, bf16[4096,1024]{1,0:T(8,128)(2,1)}, bf16[512,1024]{1,0:T(8,128)(2,1)}, bf1...) custom-call(bf16[256,4096]{1,0:T(8,128)(2,1)} %x_ref.2, ...), custom_call_target="tpu_custom_call" | custom-call | flops 99999997952 | bytes 100000000 | tf_op jit(solution)/shard_map/sum_grads/pallas_call | solution.py:439
  277.3 0.1 all-gather.4.cloned.1.call-update
  277.4 0.1 all-gather.8.cloned.1.call-start
  277.5 0.7 all-gather.8.cloned.1.call-update
  278.2 0.1 all-gather.6.cloned.1.call-start
  278.3 0.7 all-gather.6.cloned.1.call-update
  279.0 1.3 slice_bitcast_fusion
  280.3 49.9 %lamb_a.1 = (f32[4096,1024]{1,0:T(8,128)}, f32[4096,1024]{1,0:T(8,128)}, f32[4096,1024]{1,0:T(8,128)}, f32[1024,4096]{1,0:T(8,128)}, f32[1024,4096]{1,0:T(8,128)...) custom-call(f32[4096,1024]{1,0:T(8,128)} %wi.3, f32[4096,1024]{1,0:T(8,128)} %mi.3, ...), custom_call_target="tpu_custom_call" | custom-call | flops 49999998976 | bytes 136314880 | tf_op jit(solution)/shard_map/lamb_a/pallas_call | solution.py:640
  330.2 0.0 all-gather.4.cloned.1.call-done.g1
  330.2 42.8 %lamb_b.1 = (f32[1024,4096]{1,0:T(8,128)}, f32[1024,4096]{1,0:T(8,128)}, f32[1024,4096]{1,0:T(8,128)}, f32[4096,1024]{1,0:T(8,128)}, f32[4096,1024]{1,0:T(8,128)...) custom-call(f32[1024,4096]{1,0:T(8,128)} %bitcast.36, ...), custom_call_target="tpu_custom_call", output_to_operand_aliasing={{0}: (9, {}), {1}: (10, {}), {2}: (11, {})} | custom-call | flops 40000000000 | bytes 109051904 | tf_op jit(solution)/shard_map/lamb_b/pallas_call | solution.py:640
  373.0 0.0 all-gather.8.cloned.1.call-done.g2
  373.0 17.5 %lamb_c.1 = (f32[4096,1024]{1,0:T(8,128)}, f32[4096,1024]{1,0:T(8,128)}, f32[4096,1024]{1,0:T(8,128)}, f32[256,1024]{1,0:T(8,128)}) custom-call(f32[4096,1024]{1,0:T(8,128)} %bitcast.21, f32[4096,1024]{1,0:T(8,128)} %bitcast.25, f32[4096,1024]{1,0:T(8,128)} %bitcast.29, ...), custom_call_target="tpu_custom_call", output_to_operand_aliasing={{0}: (4, {}), {1}: (5, {}), {2}: (6, {})} | custom-call | flops 15000000512 | bytes 40894464 | tf_op jit(solution)/shard_map/lamb_c/pallas_call | solution.py:640
  390.5 0.0 all-gather.6.cloned.1.call-done.g2
  390.6 17.7 %lamb_d.1 = (f32[4096,1024]{1,0:T(8,128)}, f32[4096,1024]{1,0:T(8,128)}, f32[4096,1024]{1,0:T(8,128)}, f32[256,1024]{1,0:T(8,128)}, f32[8,256]{1,0:T(8,128)}) custom-call(f32[4096,1024]{1,0:T(8,128)} %bitcast.22, f32[4096,1024]{1,0:T(8,128)} %bitcast.26, f32[4096,1024]{1,0:T(8,128)} %bitcast.30, ...), custom_call_target="tpu_custom_call", output_to_operand_aliasing={{0}: (4, {}), {1}: (5, {}), {2}: (6, {})} | custom-call | flops 15000000512 | bytes 40894464 | tf_op jit(solution)/shard_map/lamb_d/pallas_call | solution.py:640
  408.3 1.3 slice.18
Async XLA Ops:
  7.2 323.0 %all-gather.4.cloned.1.call-start = ((), (), s32[]{:S(2)}) async-start(), calls=%async_computation | async-start | bytes 9437184 | tf_op jit(solution)/shard_map/all_gather | solution.py:656
  277.4 95.6 %all-gather.8.cloned.1.call-start = ((), (), s32[]{:S(2)}) async-start(), calls=%async_computation.2 | async-start | bytes 4718592 | tf_op jit(solution)/shard_map/all_gather | solution.py:656
  278.2 112.3 %all-gather.6.cloned.1.call-start = ((), (), s32[]{:S(2)}) async-start(), calls=%async_computation.1 | async-start | bytes 4718592 | tf_op jit(solution)/shard_map/all_gather | solution.py:656
Sparse Core Ops, SparseCore 0:
  277.5 48.9 all-gather.3
  328.1 28.9 all-gather.7
  358.8 28.8 all-gather.5
